TPU v7x, 512 devices: a whole 4x8x8 slice. The times are simulated.
512 devices in a mesh: dom: 64 (over z, y), feat: 8 (over x, core).
Axes of the slice: x: 4, y: 8, z: 8, core: 2. Of those that a mesh axis runs over, the one named last changes fastest.
Arguments:
- features: bfloat16 [131072, 608], P('dom', 'feat'), may hold values from -6 to 6
- weight: bfloat16 [608, 256], replicated, may hold values from -0.25 to 0.25
- out_bias: float32 [256], P('feat'), may hold values from -3 to 3
- tile_values: bfloat16 [6912, 128, 128], P('dom'), may hold values from -0.25 to 0.25
- tile_rows: int32 [6912], P('dom'), may hold values from 0 to 15
- tile_cols: int32 [6912], P('dom'), may hold values from 0 to 87, as said below
- tile_count: int32 [64], P('dom'), may hold values from 10 to 108, as said below
- send_rows: int32 [64, 8, 1024], P('dom'), may hold values from 0 to 2047
- hub_ids: int32 [1024], replicated, may hold values from 0 to 131071, as said below
Outputs:
- activations: bfloat16 [131072, 256], P('dom', 'feat')
Inputs may be any that keep to these rules, and one draw needn't show every extreme that they name: `tile_count`: slots at or past a partition's count are not part of the graph; some partition uses all 108 slots. `tile_cols`: column blocks index the extended row space of the slot's partition. `hub_ids`: distinct vertex ids; vertex v belongs to partition v // 2048; no partition owns more than 48 hubs, and some partition owns exactly 48.
All inputs are finite; a program needn't handle non-finite values.
Results may differ from a plain program's by a relative error of at most 0.0044.
Values may be sent and summed in bfloat16 or wider, within the bound.
A program may use at most 64 MiB of HBM per device.

v0:
```python
import jax
import jax.numpy as jnp
from jax import lax
from jax.sharding import PartitionSpec as P

REACH = 4
HUB_MOST = 48


def sent_to_all(shard, axis):
    copies = jnp.broadcast_to(shard, (lax.axis_size(axis), *shard.shape))
    return lax.all_to_all(copies, axis, split_axis=0, concat_axis=0, tiled=True)


def in_order(blocks, dim):
    blocks = jnp.moveaxis(blocks, 0, dim)
    dims = blocks.shape
    return blocks.reshape(*dims[:dim], dims[dim] * dims[dim + 1], *dims[dim + 2 :])


def gather_directly(shard, axis, dim):
    blocks = sent_to_all(shard, axis)
    return in_order(blocks, dim)


def passed_along(value, axis, steps):
    count = lax.axis_size(axis)
    initial, last = (max(0, -steps), min(count, count - steps))
    return lax.ppermute(value, axis, [(source, source + steps) for source in range(initial, last)])


def local(
    features, weight, out_bias, tile_values, tile_rows, tile_cols, tile_count, send_rows, hub_ids
):
    column_count = out_bias.shape[0]
    vertex_rows = features.shape[0]
    part_index = lax.axis_index("dom")
    feat_index = lax.axis_index("feat")
    weight_cols = lax.dynamic_slice_in_dim(weight, feat_index * column_count, column_count, 1)
    summed = jnp.dot(
        gather_directly(features, "feat", 1), weight_cols, preferred_element_type=jnp.float32
    )
    projected = summed.astype(jnp.bfloat16)
    half_rows = send_rows.shape[2]
    slot_total = send_rows.shape[1]
    offsets = list(range(-REACH, 0)) + list(range(1, REACH + 1))
    packed_all = projected[send_rows[0].reshape(slot_total * half_rows)].reshape(
        slot_total, half_rows, column_count
    )
    received = []
    for slot_index, offset_value in enumerate(offsets):
        received.append(passed_along(packed_all[slot_index], "dom", offset_value))
    halo_block = jnp.concatenate(received, 0)
    owners = hub_ids // vertex_rows
    mine = owners == part_index
    local_index = jnp.clip(hub_ids - part_index * vertex_rows, 0, vertex_rows - 1)
    candidates = projected[local_index]
    hub_total = hub_ids.shape[0]
    positions = jnp.arange(hub_total, dtype=jnp.int32)
    earlier = (owners[:, None] == owners[None, :]) & (positions[:, None] > positions[None, :])
    ranks = jnp.sum(earlier.astype(jnp.int32), 1)
    selector = (
        mine[:, None] & (ranks[:, None] == jnp.arange(HUB_MOST, dtype=jnp.int32)[None, :])
    ).astype(jnp.bfloat16)
    slot_rows = lax.dot_general(
        selector, candidates, (((0,), (0,)), ((), ())), preferred_element_type=jnp.float32
    ).astype(jnp.bfloat16)
    gathered = gather_directly(slot_rows, "dom", 0)
    hub_block = gathered[owners * HUB_MOST + ranks]
    extended = jnp.concatenate([projected, halo_block, hub_block], 0)
    block_edge = tile_values.shape[1]
    blocks = extended.reshape(extended.shape[0] // block_edge, block_edge, column_count)
    products = jnp.einsum(
        "tij,tjc->tic", tile_values, blocks[tile_cols], preferred_element_type=jnp.float32
    )
    live_mask = jnp.arange(tile_values.shape[0], dtype=jnp.int32) < tile_count[0]
    block_count = vertex_rows // block_edge
    assignment = (
        (tile_rows[None, :] == jnp.arange(block_count, dtype=jnp.int32)[:, None])
        & live_mask[None, :]
    ).astype(jnp.float32)
    aggregate = jnp.einsum("rt,tic->ric", assignment, products, precision=lax.Precision.HIGHEST)
    activated = jnp.maximum(aggregate + out_bias[None, None, :], 0.0).astype(jnp.bfloat16)
    return activated.reshape(vertex_rows, column_count)


def solution(mesh):
    in_specs = (
        P("dom", "feat"),
        P(),
        P("feat"),
        P("dom", None, None),
        P("dom"),
        P("dom"),
        P("dom"),
        P("dom", None, None),
        P(),
    )
    out_specs = P("dom", "feat")
    return jax.shard_map(local, mesh=mesh, in_specs=in_specs, out_specs=out_specs, check_vma=False)
```

profile of v0, /device:TPU:88, one launch (start us, length us, event | category | flops | bytes accessed | tf_op | source)
XLA Modules:
  0.0 187.9 jit_solution(9038413098160834296)
XLA Ops:
  0.0 3.0 %broadcast_in_dim.10 = bf16[8,2048,76]{1,2,0:T(8,128)(2,1)} broadcast(bf16[2048,76]{0,1:T(8,128)(2,1)} %param.9), dimensions={1,2} | broadcast | bytes 2801664 | tf_op jit(solution)/shard_map/broadcast_in_dim | solution.py:11
  3.0 4.5 %all-to-all-start = ((bf16[8,2048,76]{1,2,0:T(8,128)(2,1)}), bf16[8,2048,76]{1,2,0:T(8,128)(2,1)}, u32[]{:S(2)}, u32[]{:S(2)}) async-start(bf16[8,2048,76]{1,2,0:T(8,128)(2,1)} %broadcast_in_dim.10), calls=%async_computation | async-start | bytes 5242880 | tf_op jit(solution)/shard_map/all_to_all | solution.py:12
  13.8 26.5 %all-to-all-done = bf16[8,2048,76]{1,2,0:T(8,128)(2,1)} async-done(((bf16[8,2048,76]{1,2,0:T(8,128)(2,1)}), bf16[8,2048,76]{1,2,0:T(8,128)(2,1)}, u32[]{:S(2)}, u32[]{:S(2)}) %all-to-all-start) | async-done | bytes 2490400 | tf_op jit(solution)/shard_map/all_to_all | solution.py:12
  40.3 4.1 %reshape.67 = bf16[2048,608]{0,1:T(8,128)(2,1)} reshape(bf16[2048,8,76]{0,2,1:T(8,128)(2,1)} %bitcast.2) | data formatting | bytes 4980736 | tf_op jit(solution)/shard_map/reshape | solution.py:18
  44.5 3.1 %constant_dynamic-update-slice_fusion.9 = (bf16[11264,32]{0,1:T(8,128)(2,1)}, bf16[2048,32]{0,1:T(8,128)(2,1)}) fusion(bf16[2048,608]{0,1:T(8,128)(2,1)} %reshape.67, bf16[608,256]{1,0:T(8,128)(2,1)} %param.10, s32[]{:T(128)S(6)} %select_n.27), kind=kOutput, calls=%fused_computation.33 | convolution fusion | flops 79757312 | bytes 2908164 | tf_op jit(solution)/shard_map/dot_general | solution.py:40
  49.5 5.2 %gather_fusion.1 = bf16[1024,32]{1,0:T(8,128)(2,1)} fusion(bf16[2048,32]{1,0:T(8,128)(2,1)} %copy.50, s32[1024]{0:T(1024)S(1)} %get-tuple-element.17), kind=kCustom, calls=%fused_computation.1 | custom fusion | bytes 135168 | tf_op jit(solution)/shard_map/gather | solution.py:57
  54.7 32.0 %gather_fusion = bf16[8192,32]{1,0:T(8,128)(2,1)} fusion(bf16[2048,32]{1,0:T(8,128)(2,1)} %copy.50, s32[8192]{0:T(1024)} %broadcast_clamp_fusion), kind=kCustom, calls=%fused_computation | custom fusion | bytes 1081344 | tf_op jit(solution)/shard_map/gather | solution.py:47
  86.7 2.9 %fusion.28 = (bf16[1024,32]{1,0:T(8,128)(2,1)}, bf16[1024,32]{1,0:T(8,128)(2,1)}, bf16[1024,32]{1,0:T(8,128)(2,1)}, bf16[1024,32]{1,0:T(8,128)(2,1)}, bf16[1024,...) fusion(bf16[8192,32]{1,0:T(8,128)(2,1)} %gather_fusion), kind=kLoop, calls=%fused_computation.56 | loop fusion | bytes 1048576 | tf_op jit(solution)/shard_map/slice | solution.py:52
  91.2 4.1 %collective-permute-start = (bf16[1024,32]{0,1:T(8,128)(2,1)}, bf16[1024,32]{0,1:T(8,128)(2,1)}, u32[]{:S(2)}, u32[]{:S(2)}) collective-permute-start(bf16[1024,32]{0,1:T(8,128)(2,1)} %copy.64), channel_id=1, source_target_pairs={{32,0},{40,8},{48,16},{56,24},{64,32},{72,40},{80,48},{88,56},{96,... | collective-permute-start | bytes 196616 | tf_op jit(solution)/shard_map/ppermute | solution.py:29
  97.7 2.4 %reshape.107 = bf16[64,2,768]{2,1,0:T(2,128)(2,1)} reshape(bf16[64,32,48]{2,1,0:T(8,128)(2,1)} %broadcast_bitcast_fusion) | data formatting | bytes 393216
  100.1 14.4 %all-to-all-start.1 = ((bf16[64,2,768]{2,1,0:T(2,128)(2,1)}), bf16[64,2,768]{2,1,0:T(2,128)(2,1)}, u32[]{:S(2)}, u32[]{:S(2)}) async-start(bf16[64,2,768]{2,1,0:T(2,128)(2,1)} %reshape.107), calls=%async_computation.1 | async-start | bytes 393216 | tf_op jit(solution)/shard_map/all_to_all | solution.py:12
  126.4 2.5 %collective-permute-start.1 = (bf16[1024,32]{0,1:T(8,128)(2,1)}, bf16[1024,32]{0,1:T(8,128)(2,1)S(1)}, u32[]{:S(2)}, u32[]{:S(2)}) collective-permute-start(bf16[1024,32]{0,1:T(8,128)(2,1)} %copy.65), channel_id=1, source_target_pairs={{24,0},{32,8},{40,16},{48,24},{56,32},{64,40},{72,48},{80,56},{88,... | collective-permute-start | bytes 196616 | tf_op jit(solution)/shard_map/ppermute | solution.py:29
  128.9 5.5 %collective-permute-start.2 = (bf16[1024,32]{0,1:T(8,128)(2,1)}, bf16[1024,32]{0,1:T(8,128)(2,1)S(1)}, u32[]{:S(2)}, u32[]{:S(2)}) collective-permute-start(bf16[1024,32]{0,1:T(8,128)(2,1)} %copy.66), channel_id=1, source_target_pairs={{16,0},{24,8},{32,16},{40,24},{48,32},{56,40},{64,48},{72,56},{80,... | collective-permute-start | bytes 196616 | tf_op jit(solution)/shard_map/ppermute | solution.py:29
  134.4 3.4 %collective-permute-start.3 = (bf16[1024,32]{0,1:T(8,128)(2,1)}, bf16[1024,32]{0,1:T(8,128)(2,1)S(1)}, u32[]{:S(2)}, u32[]{:S(2)}) collective-permute-start(bf16[1024,32]{0,1:T(8,128)(2,1)} %copy.67), channel_id=1, source_target_pairs={{8,0},{16,8},{24,16},{32,24},{40,32},{48,40},{56,48},{64,56},{72,6... | collective-permute-start | bytes 196616 | tf_op jit(solution)/shard_map/ppermute | solution.py:29
  137.7 3.7 %collective-permute-start.4 = (bf16[1024,32]{0,1:T(8,128)(2,1)}, bf16[1024,32]{0,1:T(8,128)(2,1)S(1)}, u32[]{:S(2)}, u32[]{:S(2)}) collective-permute-start(bf16[1024,32]{0,1:T(8,128)(2,1)} %copy.68), channel_id=1, source_target_pairs={{0,8},{8,16},{16,24},{24,32},{32,40},{40,48},{48,56},{56,64},{64,7... | collective-permute-start | bytes 196616 | tf_op jit(solution)/shard_map/ppermute | solution.py:29
  144.8 6.6 %collective-permute-start.6 = (bf16[1024,32]{0,1:T(8,128)(2,1)}, bf16[1024,32]{0,1:T(8,128)(2,1)S(1)}, u32[]{:S(2)}, u32[]{:S(2)}) collective-permute-start(bf16[1024,32]{0,1:T(8,128)(2,1)} %copy.70), channel_id=1, source_target_pairs={{0,24},{8,32},{16,40},{24,48},{32,56},{40,64},{48,72},{56,80},{64,... | collective-permute-start | bytes 196616 | tf_op jit(solution)/shard_map/ppermute | solution.py:29
  152.1 4.6 %collective-permute-start.7 = (bf16[1024,32]{0,1:T(8,128)(2,1)}, bf16[1024,32]{0,1:T(8,128)(2,1)S(1)}, u32[]{:S(2)}, u32[]{:S(2)}) collective-permute-start(bf16[1024,32]{0,1:T(8,128)(2,1)} %copy.71), channel_id=1, source_target_pairs={{0,32},{8,40},{16,48},{24,56},{32,64},{40,72},{48,80},{56,88},{64,... | collective-permute-start | bytes 196616 | tf_op jit(solution)/shard_map/ppermute | solution.py:29
  159.9 4.1 %collective-permute-done.7 = bf16[1024,32]{0,1:T(8,128)(2,1)S(1)} collective-permute-done((bf16[1024,32]{0,1:T(8,128)(2,1)}, bf16[1024,32]{0,1:T(8,128)(2,1)S(1)}, u32[]{:S(2)}, u32[]{:S(2)}) %collective-permute-start.7) | collective-permute-done | bytes 65568 | tf_op jit(solution)/shard_map/ppermute | solution.py:29
  164.6 2.2 %reshape.108 = bf16[64,32,48]{2,1,0:T(8,128)(2,1)} reshape(bf16[64,2,768]{2,1,0:T(2,128)(2,1)} %all-to-all-done.1) | data formatting | bytes 393216
  166.8 2.2 %copy.60 = bf16[64,48,32]{2,1,0:T(8,128)(2,1)} copy(bf16[64,48,32]{1,2,0:T(8,128)(2,1)} %bitcast.36) | data formatting | bytes 393216 | tf_op jit(solution)/shard_map/all_to_all | solution.py:12
  169.1 5.3 %gather_fusion.2 = bf16[1024,32]{1,0:T(8,128)(2,1)} fusion(bf16[3072,32]{1,0:T(8,128)(2,1)} %bitcast.35, s32[1024]{0:T(1024)S(1)} %get-tuple-element.18), kind=kCustom, calls=%fused_computation.2 | custom fusion | bytes 135168 | tf_op jit(solution)/shard_map/gather | solution.py:69
  177.5 2.1 %copy_bitcast_fusion = bf16[88,128,32]{1,2,0:T(8,128)(2,1)} fusion(bf16[11264,32]{0,1:T(8,128)(2,1)} %constant_dynamic-update-slice_fusion), kind=kLoop, calls=%fused_computation.16 | loop fusion | bytes 1441792 | tf_op jit(solution)/shard_map/reshape | solution.py:72
  179.6 2.7 %gather_fusion.3 = bf16[108,128,32]{1,2,0:T(8,128)(2,1)} fusion(bf16[88,128,32]{1,2,0:T(8,128)(2,1)} %copy_bitcast_fusion, s32[1024]{0:T(1024)S(1)} %pad_clamp_fusion), kind=kCustom, calls=%fused_computation.3 | custom fusion | bytes 1769904 | tf_op jit(solution)/shard_map/gather | solution.py:74
  182.4 3.1 %convolution_bitcast_fusion = f32[108,128,32]{1,2,0:T(8,128)S(1)} fusion(bf16[108,128,32]{1,2,0:T(8,128)(2,1)} %gather_fusion.3, bf16[108,128,128]{2,1,0:T(8,128)(2,1)S(1)} %copy-done), kind=kOutput, calls=%fused_computation.11 | convolution fusion | flops 113246208 | bytes 6193152 | tf_op jit(solution)/shard_map/tij,tjc->tic/dot_general | solution.py:73
  (55 shorter events, 36.8 us)
Async XLA Ops:
  0.0 182.4 %copy-start = (bf16[108,128,128]{2,1,0:T(8,128)(2,1)S(1)}, bf16[108,128,128]{2,1,0:T(8,128)(2,1)}, u32[]{:S(2)}) copy-start(bf16[108,128,128]{2,1,0:T(8,128)(2,1)} %param.12) | copy-start | bytes 10616836
  3.0 5.2 %copy-start.6 = (s32[108]{0:T(128)S(1)}, s32[108]{0:T(128)}, u32[]{:S(2)}) copy-start(s32[108]{0:T(128)} %param.14) | copy-start | bytes 1300
  3.0 5.7 %copy-start.1 = (s32[1024]{0:T(1024)S(1)}, s32[1024]{0:T(1024)}, u32[]{:S(2)}) copy-start(s32[1024]{0:T(1024)} %param.17) | copy-start | bytes 12292
  3.0 37.3 %all-to-all-start = ((bf16[8,2048,76]{1,2,0:T(8,128)(2,1)}), bf16[8,2048,76]{1,2,0:T(8,128)(2,1)}, u32[]{:S(2)}, u32[]{:S(2)}) async-start(bf16[8,2048,76]{1,2,0:T(8,128)(2,1)} %broadcast_in_dim.10), calls=%async_computation | async-start | bytes 5242880 | tf_op jit(solution)/shard_map/all_to_all | solution.py:12
  86.7 8.7 %copy-start.2 = (pred[1024]{0:T(1024)(128)(4,1)S(1)}, pred[1024]{0:T(1024)(128)(4,1)}, u32[]{:S(2)}) copy-start(pred[1024]{0:T(1024)(128)(4,1)} %get-tuple-element.5) | copy-start | bytes 3076
  91.2 50.2 %collective-permute-start = (bf16[1024,32]{0,1:T(8,128)(2,1)}, bf16[1024,32]{0,1:T(8,128)(2,1)}, u32[]{:S(2)}, u32[]{:S(2)}) collective-permute-start(bf16[1024,32]{0,1:T(8,128)(2,1)} %copy.64), channel_id=1, source_target_pairs={{32,0},{40,8},{48,16},{56,24},{64,32},{72,40},{80,48},{88,56},{96,... | collective-permute-start | bytes 196616 | tf_op jit(solution)/shard_map/ppermute | solution.py:29
  100.1 64.5 %all-to-all-start.1 = ((bf16[64,2,768]{2,1,0:T(2,128)(2,1)}), bf16[64,2,768]{2,1,0:T(2,128)(2,1)}, u32[]{:S(2)}, u32[]{:S(2)}) async-start(bf16[64,2,768]{2,1,0:T(2,128)(2,1)} %reshape.107), calls=%async_computation.1 | async-start | bytes 393216 | tf_op jit(solution)/shard_map/all_to_all | solution.py:12
  126.4 18.4 %collective-permute-start.1 = (bf16[1024,32]{0,1:T(8,128)(2,1)}, bf16[1024,32]{0,1:T(8,128)(2,1)S(1)}, u32[]{:S(2)}, u32[]{:S(2)}) collective-permute-start(bf16[1024,32]{0,1:T(8,128)(2,1)} %copy.65), channel_id=1, source_target_pairs={{24,0},{32,8},{40,16},{48,24},{56,32},{64,40},{72,48},{80,56},{88,... | collective-permute-start | bytes 196616 | tf_op jit(solution)/shard_map/ppermute | solution.py:29
  128.9 23.2 %collective-permute-start.2 = (bf16[1024,32]{0,1:T(8,128)(2,1)}, bf16[1024,32]{0,1:T(8,128)(2,1)S(1)}, u32[]{:S(2)}, u32[]{:S(2)}) collective-permute-start(bf16[1024,32]{0,1:T(8,128)(2,1)} %copy.66), channel_id=1, source_target_pairs={{16,0},{24,8},{32,16},{40,24},{48,32},{56,40},{64,48},{72,56},{80,... | collective-permute-start | bytes 196616 | tf_op jit(solution)/shard_map/ppermute | solution.py:29
  134.4 23.0 %collective-permute-start.3 = (bf16[1024,32]{0,1:T(8,128)(2,1)}, bf16[1024,32]{0,1:T(8,128)(2,1)S(1)}, u32[]{:S(2)}, u32[]{:S(2)}) collective-permute-start(bf16[1024,32]{0,1:T(8,128)(2,1)} %copy.67), channel_id=1, source_target_pairs={{8,0},{16,8},{24,16},{32,24},{40,32},{48,40},{56,48},{64,56},{72,6... | collective-permute-start | bytes 196616 | tf_op jit(solution)/shard_map/ppermute | solution.py:29
  137.7 20.2 %collective-permute-start.4 = (bf16[1024,32]{0,1:T(8,128)(2,1)}, bf16[1024,32]{0,1:T(8,128)(2,1)S(1)}, u32[]{:S(2)}, u32[]{:S(2)}) collective-permute-start(bf16[1024,32]{0,1:T(8,128)(2,1)} %copy.68), channel_id=1, source_target_pairs={{0,8},{8,16},{16,24},{24,32},{32,40},{40,48},{48,56},{56,64},{64,7... | collective-permute-start | bytes 196616 | tf_op jit(solution)/shard_map/ppermute | solution.py:29
  141.4 17.2 %collective-permute-start.5 = (bf16[1024,32]{0,1:T(8,128)(2,1)}, bf16[1024,32]{0,1:T(8,128)(2,1)S(1)}, u32[]{:S(2)}, u32[]{:S(2)}) collective-permute-start(bf16[1024,32]{0,1:T(8,128)(2,1)} %copy.69), channel_id=1, source_target_pairs={{0,16},{8,24},{16,32},{24,40},{32,48},{40,56},{48,64},{56,72},{64,... | collective-permute-start | bytes 196616 | tf_op jit(solution)/shard_map/ppermute | solution.py:29
  144.8 14.4 %collective-permute-start.6 = (bf16[1024,32]{0,1:T(8,128)(2,1)}, bf16[1024,32]{0,1:T(8,128)(2,1)S(1)}, u32[]{:S(2)}, u32[]{:S(2)}) collective-permute-start(bf16[1024,32]{0,1:T(8,128)(2,1)} %copy.70), channel_id=1, source_target_pairs={{0,24},{8,32},{16,40},{24,48},{32,56},{40,64},{48,72},{56,80},{64,... | collective-permute-start | bytes 196616 | tf_op jit(solution)/shard_map/ppermute | solution.py:29
  152.1 11.9 %collective-permute-start.7 = (bf16[1024,32]{0,1:T(8,128)(2,1)}, bf16[1024,32]{0,1:T(8,128)(2,1)S(1)}, u32[]{:S(2)}, u32[]{:S(2)}) collective-permute-start(bf16[1024,32]{0,1:T(8,128)(2,1)} %copy.71), channel_id=1, source_target_pairs={{0,32},{8,40},{16,48},{24,56},{32,64},{40,72},{48,80},{56,88},{64,... | collective-permute-start | bytes 196616 | tf_op jit(solution)/shard_map/ppermute | solution.py:29
  182.4 3.1 %copy-start.3 = (f32[32]{0:T(128)S(1)}, f32[32]{0:T(128)}, u32[]{:S(2)}) copy-start(f32[32]{0:T(128)} %param.11) | copy-start | bytes 388
  182.4 3.1 %copy-start.4 = (s32[108]{0:T(128)S(1)}, s32[108]{0:T(128)}, u32[]{:S(2)}) copy-start(s32[108]{0:T(128)} %param.13) | copy-start | bytes 1300
  182.4 3.2 %copy-start.5 = (pred[108]{0:T(512)(128)(4,1)S(1)}, pred[108]{0:T(512)(128)(4,1)}, u32[]{:S(2)}) copy-start(pred[108]{0:T(512)(128)(4,1)} %iota_compare_fusion.3) | copy-start | bytes 328
where the time goes:
time: 190 us; the launch traced here: 188 us
  local copies, waits for them, and re-layouts  91.6 us (48%)
  starting transfers between devices  51.2 us (27%)
  waiting for transfers between devices  30.6 us (16%)
  matrix products  9.47 us (5%)
  other arithmetic  4.19 us (2%)
    ppermute x8, starting transfers between devices, passed_along(): lax.ppermute(value, axis, [(source, source + steps) for source in range(i...  32.2 us
    gather x1, local copies, waits for them, and re-layouts, local(): projected[send_rows[0].reshape(slot_total * half_rows)]  32 us
    unnamed x35, local copies, waits for them, and re-layouts  27.1 us
    all_to_all x2, waiting for transfers between devices, sent_to_all(): return lax.all_to_all(copies, axis, split_axis=0, concat_axis=0, tiled=True)  26.5 us
    all_to_all x2, starting transfers between devices, sent_to_all(): return lax.all_to_all(copies, axis, split_axis=0, concat_axis=0, tiled=True)  19 us
    gather x2, local copies, waits for them, and re-layouts, local(): hub_block = gathered[owners * HUB_MOST + ranks]  6.99 us
    gather x1, local copies, waits for them, and re-layouts, local(): candidates = projected[local_index]  5.18 us
    reshape x1, local copies, waits for them, and re-layouts, in_order(): blocks.reshape(*dims[:dim], dims[dim] * dims[dim + 1], *dims[dim + 2:])  4.14 us
  transfers between devices with their start and end apart: 10, of which 2 were waited for; matrix products, arithmetic and copies ran while one was open for 15% of the time, Pallas kernels for 0%

commit v1 on v0

v1 whole, which is shorter than its diff:
```python
import functools

import jax
import jax.numpy as jnp
from jax import lax
from jax.experimental import pallas as pl
from jax.experimental.pallas import tpu as pltpu
from jax.sharding import PartitionSpec as P

REACH = 4
HUB_MOST = 48
Y_RING = 8
LO = 256
BLK = 128
OFFSETS = tuple(range(-REACH, 0)) + tuple(range(1, REACH + 1))
SEND_ORDER = (0, 7, 1, 6, 2, 5, 3, 4)
MESH = pl.DeviceIdType.MESH
F32, BF16, I32 = jnp.float32, jnp.bfloat16, jnp.int32


def dims(a, b):
    return (((a,), (b,)), ((), ()))


def dot(a, b, ca=1, cb=0):
    return lax.dot_general(a, b, dims(ca, cb), preferred_element_type=F32)


def ones_where(mask):
    return jnp.where(mask, 1.0, 0.0).astype(BF16)


def pick_groups(stacked, group_of, groups, height):
    total = None
    for g in range(groups):
        part = jnp.where(group_of == g, stacked[g * height : (g + 1) * height], 0.0)
        total = part if total is None else total + part
    return total


def exchange_kernel(
    n_dom, n_feat, cols, chunk,
    ft_ref, w_ref, send_ref, hub_ref, ext_ref,
    part_ref, hot_ref, hubhot_ref, endhot_ref, sx, rx, sy, hub_out, hy, hpack, hz,
    sxs, sxr, sys_, syr, hys, hyr, hzs, hzr,
):
    p = lax.axis_index("dom")
    j = lax.axis_index("feat")
    y = lax.rem(p, Y_RING)
    z = lax.div(p, Y_RING)
    z_ring = n_dom // Y_RING
    k_in, rows = ft_ref.shape
    hid = w_ref.shape[1]
    n_chunk = cols // chunk
    his = rows // LO
    halo = send_ref.shape[1]
    own_blocks = rows // BLK
    slot_blocks = halo // BLK
    hub_first = own_blocks + len(OFFSETS) * slot_blocks

    def dom_at(step):
        return lax.rem(p + step + n_dom, n_dom)

    def y_at(step):
        return z * Y_RING + lax.rem(y + step, Y_RING)

    def z_at(step):
        return lax.rem(z + step, z_ring) * Y_RING + y

    def feat_at(step):
        return lax.rem(j + step, n_feat)

    barrier = pltpu.get_barrier_semaphore()
    greeted = 0
    for d in range(1, n_feat):
        pl.semaphore_signal(barrier, inc=1, device_id={"feat": feat_at(d)}, device_id_type=MESH)
        greeted += 1
    for o in OFFSETS:
        pl.semaphore_signal(barrier, inc=1, device_id={"dom": dom_at(o)}, device_id_type=MESH)
        greeted += 1
    for d in range(1, Y_RING):
        pl.semaphore_signal(barrier, inc=1, device_id={"dom": y_at(d)}, device_id_type=MESH)
        greeted += 1
    for d in range(1, z_ring):
        pl.semaphore_signal(barrier, inc=1, device_id={"dom": z_at(d)}, device_id_type=MESH)
        greeted += 1

    f_in = w_ref.shape[0]
    pick = ones_where(
        lax.broadcasted_iota(I32, (BLK, f_in), 1)
        == lax.broadcasted_iota(I32, (BLK, f_in), 0) + j * k_in
    )
    w_mine = dot(pick, w_ref[...])
    w_t = w_mine.T.astype(BF16)[:, :k_in]
    ft = ft_ref[...]

    def partials(h):
        left = jnp.concatenate(
            [w_t[d * cols + h * chunk : d * cols + (h + 1) * chunk] for d in range(n_feat)], 0
        )
        part = dot(left, ft)
        for d in range(n_feat):
            block = part[d * chunk : (d + 1) * chunk]
            part_ref[d, h * chunk : (h + 1) * chunk, :] = block
            sx[d, h] = block.astype(BF16)

    for h in range(n_chunk):
        partials(h)

    pl.semaphore_wait(barrier, greeted)

    x_copies = {}
    for h in range(n_chunk):
        for d in range(1, n_feat):
            x_copies[h, d] = pltpu.make_async_remote_copy(
                src_ref=sx.at[feat_at(d), h],
                dst_ref=rx.at[h, d - 1],
                send_sem=sxs.at[h, d - 1],
                recv_sem=sxr.at[h, d - 1],
                device_id={"feat": feat_at(d)},
                device_id_type=MESH,
            )
            x_copies[h, d].start()

    for s in range(len(OFFSETS)):
        lo = lax.rem(send_ref[s : s + 1, :], LO)
        hot_ref[s] = ones_where(lax.broadcasted_iota(I32, (LO, halo), 0) == lo)

    ids = hub_ref[...]
    hubs = ids.shape[1]
    owner = lax.div(ids, rows)
    local_row = lax.rem(ids, rows)
    owned = lax.broadcasted_iota(I32, (n_dom, hubs), 0) == owner
    before = ones_where(
        lax.broadcasted_iota(I32, (hubs, hubs), 0) < lax.broadcasted_iota(I32, (hubs, hubs), 1)
    )
    earlier = dot(ones_where(owned), before)
    rank = jnp.sum(jnp.where(owned, earlier, 0.0), 0, keepdims=True).astype(I32)
    place = lax.rem(rank + y * HUB_MOST, BLK)
    taken = ones_where(
        (lax.broadcasted_iota(I32, (BLK, hubs), 0) == place) & (owner == p)
    )
    halves = jnp.concatenate(
        [lax.rem(local_row, LO).astype(F32), (lax.div(local_row, LO) + 1).astype(F32)]
        + [jnp.zeros((14, hubs), F32)],
        0,
    ).astype(BF16)
    listed = dot(halves, taken, 1, 1)
    hub_lo = listed[0:1].astype(I32)
    hub_hi = listed[1:2].astype(I32) - 1
    hubhot_ref[...] = ones_where(lax.broadcasted_iota(I32, (LO, BLK), 0) == hub_lo)
    packed = Y_RING * HUB_MOST
    end_place = lax.rem(owner, Y_RING) * HUB_MOST + rank
    end_z = lax.div(owner, Y_RING)
    endhot_ref[...] = ones_where(lax.broadcasted_iota(I32, (packed, hubs), 0) == end_place)

    started = []
    hub_copies = {}
    for h in range(n_chunk):
        span = slice(h * chunk, (h + 1) * chunk)
        for d in range(1, n_feat):
            x_copies[h, d].wait()
        total = part_ref[j, span, :]
        for d in range(1, n_feat):
            total = total + rx[h, d - 1].astype(F32)
        proj = total.astype(BF16)
        for b in range(own_blocks):
            ext_ref[b, span, :] = proj[:, b * BLK : (b + 1) * BLK]
        stacked = jnp.concatenate([proj[:, g * LO : (g + 1) * LO] for g in range(his)], 0)

        mine = pick_groups(dot(stacked, hubhot_ref[...]), hub_hi, his, chunk).astype(BF16)
        hub_out[h] = mine
        hy[h, y] = mine
        for d in range(1, Y_RING):
            hub_copies[h, d] = pltpu.make_async_remote_copy(
                src_ref=hub_out.at[h],
                dst_ref=hy.at[h, y],
                send_sem=hys.at[h, d - 1],
                recv_sem=hyr.at[h, d - 1],
                device_id={"dom": y_at(d)},
                device_id_type=MESH,
            )
            hub_copies[h, d].start()

        for s in SEND_ORDER:
            target = p + OFFSETS[s]
            here = (target >= 0) & (target < n_dom)
            hi = jnp.where(here, lax.div(send_ref[s : s + 1, :], LO), -1)
            rows_out = pick_groups(dot(stacked, hot_ref[s]), hi, his, chunk).astype(BF16)
            for b in range(slot_blocks):
                sy[h, s, b] = rows_out[:, b * BLK : (b + 1) * BLK]
            first = own_blocks + s * slot_blocks
            copy = pltpu.make_async_remote_copy(
                src_ref=sy.at[h, s],
                dst_ref=ext_ref.at[first : first + slot_blocks, span, :],
                send_sem=sys_.at[h, s],
                recv_sem=syr.at[h, s],
                device_id={"dom": dom_at(OFFSETS[s])},
                device_id_type=MESH,
            )
            copy.start()
            started.append(copy)

    for h in range(n_chunk):
        for d in range(1, Y_RING):
            hub_copies[h, d].wait()
        for t in range(packed // BLK):
            lane = lax.broadcasted_iota(I32, (chunk, BLK), 1) + t * BLK
            tile = jnp.zeros((chunk, BLK), F32)
            for source in range(Y_RING):
                low, high = source * HUB_MOST, (source + 1) * HUB_MOST
                if high <= t * BLK or low >= (t + 1) * BLK:
                    continue
                tile = jnp.where((lane >= low) & (lane < high), hy[h, source].astype(F32), tile)
            hpack[h * chunk : (h + 1) * chunk, t * BLK : (t + 1) * BLK] = tile.astype(BF16)
    hz[z] = hpack[...]
    z_copies = []
    for d in range(1, z_ring):
        copy = pltpu.make_async_remote_copy(
            src_ref=hpack,
            dst_ref=hz.at[z],
            send_sem=hzs.at[d - 1],
            recv_sem=hzr.at[d - 1],
            device_id={"dom": z_at(d)},
            device_id_type=MESH,
        )
        copy.start()
        z_copies.append(copy)
    for copy in z_copies:
        copy.wait()
    everyone = jnp.concatenate([hz[source] for source in range(z_ring)], 0)
    hub_block = pick_groups(dot(everyone, endhot_ref[...]), end_z, z_ring, cols).astype(BF16)
    for b in range(hubs // BLK):
        ext_ref[hub_first + b] = hub_block[:, b * BLK : (b + 1) * BLK]

    for copy in started:
        copy.wait()


def tile_kernel(rows_ref, cols_ref, count_ref, tiles_ref, ext_ref, bias_ref, out_ref, acc_ref):
    live = count_ref[0]
    row_blocks = acc_ref.shape[0] - 1
    columns = acc_ref.shape[1]
    acc_ref[...] = jnp.zeros_like(acc_ref)
    unroll = 4

    @pl.loop(0, tiles_ref.shape[0] // unroll)
    def _(step):
        products = []
        for u in range(unroll):
            t = step * unroll + u
            products.append(dot(ext_ref[cols_ref[t]], tiles_ref[t], 1, 1))
        for u in range(unroll):
            t = step * unroll + u
            row = jnp.where(t < live, rows_ref[t], row_blocks)
            acc_ref[row] += products[u]

    eye = lax.broadcasted_iota(I32, (columns, columns), 0) == lax.broadcasted_iota(
        I32, (columns, columns), 1
    )
    bias = jnp.sum(jnp.where(eye, bias_ref[...], 0.0), 1, keepdims=True)
    for b in range(row_blocks):
        out_ref[:, b * BLK : (b + 1) * BLK] = jnp.maximum(acc_ref[b] + bias, 0.0).astype(BF16)


def local(
    n_dom, n_feat,
    features, weight, out_bias, tile_values, tile_rows, tile_cols, tile_count, send_rows, hub_ids,
):
    rows, _ = features.shape
    cols = out_bias.shape[0]
    hid = weight.shape[1]
    hubs = hub_ids.shape[0]
    slots, halo = send_rows.shape[1:]
    chunk = 16
    n_chunk = cols // chunk
    z_ring = n_dom // Y_RING
    blocks = (rows + slots * halo + hubs) // BLK
    vmem = pl.BlockSpec(memory_space=pltpu.VMEM)
    smem = pl.BlockSpec(memory_space=pltpu.SMEM)
    dma = pltpu.SemaphoreType.DMA
    extended = pl.pallas_call(
        functools.partial(exchange_kernel, n_dom, n_feat, cols, chunk),
        out_shape=jax.ShapeDtypeStruct((blocks, cols, BLK), BF16),
        in_specs=[vmem] * 4,
        out_specs=vmem,
        scratch_shapes=[
            pltpu.VMEM((n_feat, cols, rows), F32),
            pltpu.VMEM((slots, LO, halo), BF16),
            pltpu.VMEM((LO, BLK), BF16),
            pltpu.VMEM((Y_RING * HUB_MOST, hubs), BF16),
            pltpu.VMEM((n_feat, n_chunk, chunk, rows), BF16),
            pltpu.VMEM((n_chunk, n_feat - 1, chunk, rows), BF16),
            pltpu.VMEM((n_chunk, slots, halo // BLK, chunk, BLK), BF16),
            pltpu.VMEM((n_chunk, chunk, BLK), BF16),
            pltpu.VMEM((n_chunk, Y_RING, chunk, BLK), BF16),
            pltpu.VMEM((cols, Y_RING * HUB_MOST), BF16),
            pltpu.VMEM((z_ring, cols, Y_RING * HUB_MOST), BF16),
            dma((n_chunk, n_feat - 1)),
            dma((n_chunk, n_feat - 1)),
            dma((n_chunk, slots)),
            dma((n_chunk, slots)),
            dma((n_chunk, Y_RING - 1)),
            dma((n_chunk, Y_RING - 1)),
            dma((z_ring - 1,)),
            dma((z_ring - 1,)),
        ],
        compiler_params=pltpu.CompilerParams(
            collective_id=0, has_side_effects=True, vmem_limit_bytes=40 * 2**20
        ),
        name="exchange",
    )(features.T, weight, send_rows[0], hub_ids[None, :])
    out_t = pl.pallas_call(
        tile_kernel,
        out_shape=jax.ShapeDtypeStruct((cols, rows), BF16),
        in_specs=[smem, smem, smem, vmem, vmem, vmem],
        out_specs=vmem,
        scratch_shapes=[pltpu.VMEM((rows // BLK + 1, cols, BLK), F32)],
        name="tiles",
    )(tile_rows, tile_cols, tile_count, tile_values, extended, out_bias[None, :])
    return out_t.T


def solution(mesh):
    in_specs = (
        P("dom", "feat"),
        P(),
        P("feat"),
        P("dom", None, None),
        P("dom"),
        P("dom"),
        P("dom"),
        P("dom", None, None),
        P(),
    )
    out_specs = P("dom", "feat")
    body = functools.partial(local, mesh.shape["dom"], mesh.shape["feat"])
    return jax.shard_map(body, mesh=mesh, in_specs=in_specs, out_specs=out_specs, check_vma=False)
```

time: 190 us -> 59.6 us (0.31)
  the two profiles are of different devices: /device:TPU:88 before, /device:TPU:1 now
where the time goes in v1:
time: 59.6 us; the launch traced here: 59.3 us
  Pallas kernels  54.4 us (91%)
  local copies, waits for them, and re-layouts  4.23 us (7%)
  between operations  0.68 us (1%)
    pallas_call x1, Pallas kernels, local(): pl.pallas_call(functools.partial(exchange_kernel, n_dom, n_feat, cols, ch...  46.3 us
    pallas_call x1, Pallas kernels, local(): pl.pallas_call(tile_kernel, out_shape=jax.ShapeDtypeStruct((cols, rows),...  8.05 us
    unnamed x10, local copies, waits for them, and re-layouts  4.23 us

profile of v1, /device:TPU:1, one launch (start us, length us, event | category | flops | bytes accessed | tf_op | source)
XLA Modules:
  0.0 59.3 jit_solution(8923060618296609972)
XLA Ops:
  0.7 0.0 copy-start.1
  0.7 1.0 %copy-done.1 = bf16[2048,76]{0,1:T(8,128)(2,1)S(1)} copy-done((bf16[2048,76]{0,1:T(8,128)(2,1)S(1)}, bf16[2048,76]{0,1:T(8,128)(2,1)}, u32[]{:S(2)}) %copy-start.1) | copy-done | bytes 311320
  1.6 0.0 copy-start.2
  1.6 1.0 %copy-done.2 = bf16[608,256]{1,0:T(8,128)(2,1)S(1)} copy-done((bf16[608,256]{1,0:T(8,128)(2,1)S(1)}, bf16[608,256]{1,0:T(8,128)(2,1)}, u32[]{:S(2)}) %copy-start.2) | copy-done | bytes 311320
  2.6 0.0 copy-start.3
  2.6 0.8 %copy-done.3 = s32[1,8,1024]{2,1,0:T(8,128)S(1)} copy-done((s32[1,8,1024]{2,1,0:T(8,128)S(1)}, s32[1,8,1024]{2,1,0:T(8,128)}, u32[]{:S(2)}) %copy-start.3) | copy-done | bytes 32792
  3.4 0.0 copy-start.4
  3.4 0.7 %copy-done.4 = s32[1024]{0:T(1024)S(1)} copy-done((s32[1024]{0:T(1024)S(1)}, s32[1024]{0:T(1024)}, u32[]{:S(2)}) %copy-start.4) | copy-done | bytes 4120
  4.0 46.3 %exchange.1.ext_ref = bf16[88,32,128]{2,1,0:T(8,128)(2,1)S(1)} custom-call(bf16[76,2048]{1,0:T(8,128)(2,1)S(1)} %bitcast.5, bf16[608,256]{1,0:T(8,128)(2,1)S(1)} %copy-done.2, s32[8,1024]{1,0:T(8,128)S(1)} %bitcast.6, s32[1,1024]{1,0:T(1,128)S(1)} %bitcast.7), custom_call_target="tpu_custom_call" | custom-call | tf_op jit(solution)/shard_map/exchange/pallas_call | solution.py:282
  50.4 0.0 copy-start
  50.4 0.9 %copy-done = bf16[88,32,128]{2,1,0:T(8,128)(2,1)} copy-done((bf16[88,32,128]{2,1,0:T(8,128)(2,1)}, bf16[88,32,128]{2,1,0:T(8,128)(2,1)S(1)}, u32[]{:S(2)}) %copy-start) | copy-done | bytes 720920
  51.2 8.1 %tiles.1 = bf16[32,2048]{1,0:T(8,128)(2,1)} custom-call(s32[108]{0:T(128)} %rows_ref.1, s32[108]{0:T(128)} %cols_ref.1, s32[1]{0:T(128)S(6)} %copy.10.count_ref, bf16[108,128,128]{2,1,0:T(8,128)(2,1)} %tiles_ref.1, bf16[88,32,128]{2,1,0:T(8,128)(2,1)} %copy-done, f32[1,32]{1,0:T(1,128)} %bitcast.8), custom_call_target="tpu_custom_call" | custom-call | tf_op jit(solution)/shard_map/tiles/pallas_call | solution.py:313
Async XLA Ops:
  0.7 1.0 %copy-start.1 = (bf16[2048,76]{0,1:T(8,128)(2,1)S(1)}, bf16[2048,76]{0,1:T(8,128)(2,1)}, u32[]{:S(2)}) copy-start(bf16[2048,76]{0,1:T(8,128)(2,1)} %param.9) | copy-start | bytes 933892
  1.6 1.0 %copy-start.2 = (bf16[608,256]{1,0:T(8,128)(2,1)S(1)}, bf16[608,256]{1,0:T(8,128)(2,1)}, u32[]{:S(2)}) copy-start(bf16[608,256]{1,0:T(8,128)(2,1)} %w_ref.1) | copy-start | bytes 933892
  2.6 0.8 %copy-start.3 = (s32[1,8,1024]{2,1,0:T(8,128)S(1)}, s32[1,8,1024]{2,1,0:T(8,128)}, u32[]{:S(2)}) copy-start(s32[1,8,1024]{2,1,0:T(8,128)} %param.16) | copy-start | bytes 98308
  3.4 0.7 %copy-start.4 = (s32[1024]{0:T(1024)S(1)}, s32[1024]{0:T(1024)}, u32[]{:S(2)}) copy-start(s32[1024]{0:T(1024)} %param.17) | copy-start | bytes 12292
  50.4 0.9 %copy-start = (bf16[88,32,128]{2,1,0:T(8,128)(2,1)}, bf16[88,32,128]{2,1,0:T(8,128)(2,1)S(1)}, u32[]{:S(2)}) copy-start(bf16[88,32,128]{2,1,0:T(8,128)(2,1)S(1)} %exchange.1.ext_ref) | copy-start | bytes 2162692

commit v2 on v1

v2 whole, which is shorter than its diff:
```python
import functools

import jax
import jax.numpy as jnp
from jax import lax
from jax.experimental import pallas as pl
from jax.experimental.pallas import tpu as pltpu
from jax.sharding import PartitionSpec as P

REACH = 4
HUB_MOST = 48
Y_RING = 8
LO = 256
BLK = 128
OFFSETS = tuple(range(-REACH, 0)) + tuple(range(1, REACH + 1))
SEND_ORDER = (0, 7, 1, 6, 2, 5, 3, 4)
VMEM_MOST = 67_043_328
MESH = pl.DeviceIdType.MESH
F32, BF16, I32 = jnp.float32, jnp.bfloat16, jnp.int32


def dims(a, b):
    return (((a,), (b,)), ((), ()))


def dot(a, b, ca=1, cb=0):
    return lax.dot_general(a, b, dims(ca, cb), preferred_element_type=F32)


def ones_where(mask):
    return jnp.where(mask, 1.0, 0.0).astype(BF16)


def pick_groups(stacked, group_of, groups, height):
    total = None
    for g in range(groups):
        part = jnp.where(group_of == g, stacked[g * height : (g + 1) * height], 0.0)
        total = part if total is None else total + part
    return total


def exchange_kernel(
    n_dom, n_feat, cols, chunk,
    ft_hbm, w_hbm, send_hbm, hub_hbm, tiles_hbm, rows_hbm, cols_hbm, count_hbm, bias_hbm,
    ext_ref, tiles_ref, meta_ref, bias_ref,
    ft_ref, w_ref, send_ref, hub_ref, hot_ref, endhot_ref, sx, rx, sy,
    hx_out, hx, hub_out, hy, hpack, hz, meta_in, count_in, bias_in,
    in_sem, sxs, sxr, sys_, syr, hxs, hxr, hys, hyr, hzs, hzr, feat_in, near_in, ring_in,
):
    p = lax.axis_index("dom")
    j = lax.axis_index("feat")
    y = lax.rem(p, Y_RING)
    z = lax.div(p, Y_RING)
    z_ring = n_dom // Y_RING
    k_in, rows = ft_ref.shape
    n_chunk = cols // chunk
    his = rows // LO
    slots, halo = send_ref.shape
    own_blocks = rows // BLK
    slot_blocks = halo // BLK
    hub_first = own_blocks + slots * slot_blocks
    near_desk, ring_desk = n_feat - 1, n_feat - 2

    loads = []
    for i, (src, dst) in enumerate(
        (
            (hub_hbm, hub_ref), (ft_hbm, ft_ref), (w_hbm, w_ref), (send_hbm, send_ref),
            (rows_hbm, meta_in.at[0]), (cols_hbm, meta_in.at[1]),
            (count_hbm, count_in), (bias_hbm, bias_in), (tiles_hbm, tiles_ref),
        )
    ):
        loads.append(pltpu.make_async_copy(src, dst, in_sem.at[i]))
        loads[-1].start()

    def y_at(step):
        return z * Y_RING + lax.rem(y + step, Y_RING)

    def z_at(step):
        return lax.rem(z + step, z_ring) * Y_RING + y

    def feat_at(step):
        return lax.rem(j + step, n_feat)

    def tell(sem, dom, feat):
        pl.semaphore_signal(
            sem, inc=1, device_id={"dom": dom, "feat": feat}, device_id_type=MESH
        )

    def inside(o):
        return (p + o >= 0) & (p + o < n_dom)

    barrier = pltpu.get_barrier_semaphore()
    for other in range(ring_desk):

        @pl.when(j != other)
        def _():
            tell(barrier, p, other)

    loads[0].wait()
    ids = hub_ref[...]
    hubs = ids.shape[1]
    owner = lax.div(ids, rows)
    local_row = lax.rem(ids, rows)
    owned = lax.broadcasted_iota(I32, (n_dom, hubs), 0) == owner
    before = ones_where(
        lax.broadcasted_iota(I32, (hubs, hubs), 0) < lax.broadcasted_iota(I32, (hubs, hubs), 1)
    )
    earlier = dot(ones_where(owned), before)
    rank = jnp.sum(jnp.where(owned, earlier, 0.0), 0, keepdims=True).astype(I32)
    place = lax.rem(rank + y * HUB_MOST, BLK)
    taken = ones_where((lax.broadcasted_iota(I32, (BLK, hubs), 0) == place) & (owner == p))
    halves = jnp.concatenate(
        [lax.rem(local_row, LO).astype(F32), (lax.div(local_row, LO) + 1).astype(F32)]
        + [jnp.zeros((14, hubs), F32)],
        0,
    ).astype(BF16)
    listed = dot(halves, taken, 1, 1)
    hub_row = (listed[0:1] + LO * (listed[1:2] - 1.0)).astype(I32)
    hub_pick = ones_where(lax.broadcasted_iota(I32, (rows, BLK), 0) == hub_row)

    f_in = w_ref.shape[0]
    loads[2].wait()
    pick = ones_where(
        lax.broadcasted_iota(I32, (BLK, f_in), 1)
        == lax.broadcasted_iota(I32, (BLK, f_in), 0) + j * k_in
    )
    w_mine = dot(pick, w_ref[...])
    w_t = w_mine.T.astype(BF16)[:, :k_in]

    loads[1].wait()
    ft = ft_ref[...]
    hub_ft = dot(ft, hub_pick).astype(BF16)
    hub_part = dot(w_t, hub_ft).astype(BF16)
    for d in range(n_feat):
        hx_out[d] = hub_part[d * cols : (d + 1) * cols]

    @pl.when(j < ring_desk)
    def _():
        pl.semaphore_wait(barrier, n_feat - 1)

    @pl.when(j == 0)
    def _():
        tell(feat_in, p, near_desk)
        tell(feat_in, p, ring_desk)

    @pl.when(j >= ring_desk)
    def _():
        pl.semaphore_wait(feat_in, 1)

    @pl.when(j == near_desk)
    def _():
        for o in OFFSETS:

            @pl.when(inside(o))
            def _():
                tell(barrier, p + o, near_desk)

        for d in range(1, Y_RING):
            tell(barrier, y_at(d), near_desk)

    @pl.when(j == ring_desk)
    def _():
        for d in range(1, z_ring):
            tell(barrier, z_at(d), ring_desk)

    hub_x = []
    for d in range(1, n_feat):
        copy = pltpu.make_async_remote_copy(
            src_ref=hx_out.at[feat_at(d)],
            dst_ref=hx.at[d - 1],
            send_sem=hxs.at[d - 1],
            recv_sem=hxr.at[d - 1],
            device_id={"feat": feat_at(d)},
            device_id_type=MESH,
        )
        copy.start()
        hub_x.append(copy)

    x_copies = {}
    for h in range(n_chunk):
        left = jnp.concatenate(
            [w_t[d * cols + h * chunk : d * cols + (h + 1) * chunk] for d in range(n_feat)], 0
        )
        part = dot(left, ft).astype(BF16)
        for d in range(n_feat):
            sx[d, h] = part[d * chunk : (d + 1) * chunk]
        for d in range(1, n_feat):
            x_copies[h, d] = pltpu.make_async_remote_copy(
                src_ref=sx.at[feat_at(d), h],
                dst_ref=rx.at[h, d - 1],
                send_sem=sxs.at[h, d - 1],
                recv_sem=sxr.at[h, d - 1],
                device_id={"feat": feat_at(d)},
                device_id_type=MESH,
            )
            x_copies[h, d].start()

    for copy in hub_x:
        copy.wait()
    hub_sum = hx_out[j].astype(F32)
    for d in range(1, n_feat):
        hub_sum = hub_sum + hx[d - 1].astype(F32)
    hub_mine = hub_sum.astype(BF16)
    hub_out[...] = hub_mine
    hy[y] = hub_mine

    @pl.when(j == near_desk)
    def _():
        before_p = lax.min(p, REACH)
        after_p = lax.min(n_dom - 1 - p, REACH)
        pl.semaphore_wait(barrier, before_p + after_p + Y_RING - 1)
        for other in range(n_feat - 1):
            tell(near_in, p, other)

    @pl.when(j != near_desk)
    def _():
        pl.semaphore_wait(near_in, 1)

    hub_y = []
    for d in range(1, Y_RING):
        copy = pltpu.make_async_remote_copy(
            src_ref=hub_out,
            dst_ref=hy.at[y],
            send_sem=hys.at[d - 1],
            recv_sem=hyr.at[d - 1],
            device_id={"dom": y_at(d)},
            device_id_type=MESH,
        )
        copy.start()
        hub_y.append(copy)

    loads[3].wait()
    for s in range(slots):
        lo = lax.rem(send_ref[s : s + 1, :], LO)
        hot_ref[s] = ones_where(lax.broadcasted_iota(I32, (LO, halo), 0) == lo)
    packed = Y_RING * HUB_MOST
    end_place = lax.rem(owner, Y_RING) * HUB_MOST + rank
    end_z = lax.div(owner, Y_RING)
    endhot_ref[...] = ones_where(lax.broadcasted_iota(I32, (packed, hubs), 0) == end_place)

    for i in range(4, 8):
        loads[i].wait()
    tiles = meta_in.shape[2]
    live = lax.broadcasted_iota(I32, (1, tiles), 1) < count_in[0]
    meta_ref[0:1, 0:tiles] = jnp.where(live, meta_in[0], own_blocks)
    meta_ref[1:2, 0:tiles] = meta_in[1]
    eye = lax.broadcasted_iota(I32, (cols, cols), 0) == lax.broadcasted_iota(I32, (cols, cols), 1)
    bias = jnp.sum(jnp.where(eye, bias_in[...], 0.0), 1, keepdims=True)
    bias_ref[...] = jnp.broadcast_to(bias, (cols, BLK))

    for s in range(slots):

        @pl.when(jnp.logical_not(inside(-OFFSETS[s])))
        def _():
            first = own_blocks + s * slot_blocks
            ext_ref[first : first + slot_blocks] = jnp.zeros((slot_blocks, cols, BLK), BF16)

    y_copies = {}

    def bulk(h):
        span = slice(h * chunk, (h + 1) * chunk)
        for d in range(1, n_feat):
            x_copies[h, d].wait()
        total = sx[j, h].astype(F32)
        for d in range(1, n_feat):
            total = total + rx[h, d - 1].astype(F32)
        proj = total.astype(BF16)
        for b in range(own_blocks):
            ext_ref[b, span, :] = proj[:, b * BLK : (b + 1) * BLK]
        stacked = jnp.concatenate([proj[:, g * LO : (g + 1) * LO] for g in range(his)], 0)
        for s in SEND_ORDER:
            hi = lax.div(send_ref[s : s + 1, :], LO)
            rows_out = pick_groups(dot(stacked, hot_ref[s]), hi, his, chunk).astype(BF16)
            for b in range(slot_blocks):
                sy[h, s, b] = rows_out[:, b * BLK : (b + 1) * BLK]
            first = own_blocks + s * slot_blocks
            y_copies[h, s] = pltpu.make_async_remote_copy(
                src_ref=sy.at[h, s],
                dst_ref=ext_ref.at[first : first + slot_blocks, span, :],
                send_sem=sys_.at[h, s],
                recv_sem=syr.at[h, s],
                device_id={"dom": p + OFFSETS[s]},
                device_id_type=MESH,
            )

            @pl.when(inside(OFFSETS[s]))
            def _():
                y_copies[h, s].start()

    bulk(0)

    for copy in hub_y:
        copy.wait()
    for t in range(packed // BLK):
        lane = lax.broadcasted_iota(I32, (cols, BLK), 1) + t * BLK
        tile = jnp.zeros((cols, BLK), F32)
        for source in range(Y_RING):
            low, high = source * HUB_MOST, (source + 1) * HUB_MOST
            if high <= t * BLK or low >= (t + 1) * BLK:
                continue
            tile = jnp.where((lane >= low) & (lane < high), hy[source].astype(F32), tile)
        hpack[:, t * BLK : (t + 1) * BLK] = tile.astype(BF16)
    hz[z] = hpack[...]

    @pl.when(j == ring_desk)
    def _():
        pl.semaphore_wait(barrier, z_ring - 1)
        for other in range(n_feat):
            if other != ring_desk:
                tell(ring_in, p, other)

    @pl.when(j != ring_desk)
    def _():
        pl.semaphore_wait(ring_in, 1)

    hub_z = []
    for d in range(1, z_ring):
        copy = pltpu.make_async_remote_copy(
            src_ref=hpack,
            dst_ref=hz.at[z],
            send_sem=hzs.at[d - 1],
            recv_sem=hzr.at[d - 1],
            device_id={"dom": z_at(d)},
            device_id_type=MESH,
        )
        copy.start()
        hub_z.append(copy)

    for h in range(1, n_chunk):
        bulk(h)

    for copy in hub_z:
        copy.wait()
    everyone = jnp.concatenate([hz[source] for source in range(z_ring)], 0)
    hub_block = pick_groups(dot(everyone, endhot_ref[...]), end_z, z_ring, cols).astype(BF16)
    for b in range(hubs // BLK):
        ext_ref[hub_first + b] = hub_block[:, b * BLK : (b + 1) * BLK]

    loads[8].wait()
    for (h, s), copy in y_copies.items():

        @pl.when(inside(OFFSETS[s]))
        def _():
            copy.wait_send()

        @pl.when(inside(-OFFSETS[s]))
        def _():
            copy.wait_recv()


def tile_kernel(meta_ref, tiles_ref, ext_ref, bias_ref, out_ref, acc_ref):
    row_blocks = acc_ref.shape[0] - 1
    acc_ref[...] = jnp.zeros_like(acc_ref)
    unroll = 6

    @pl.loop(0, tiles_ref.shape[0] // unroll)
    def _(step):
        products = []
        for u in range(unroll):
            t = step * unroll + u
            products.append(dot(ext_ref[meta_ref[1, t]], tiles_ref[t], 1, 1))
        for u in range(unroll):
            acc_ref[meta_ref[0, step * unroll + u]] += products[u]

    bias = bias_ref[...]
    for b in range(row_blocks):
        out_ref[:, b * BLK : (b + 1) * BLK] = jnp.maximum(acc_ref[b] + bias, 0.0).astype(BF16)


def local(
    n_dom, n_feat,
    features, weight, out_bias, tile_values, tile_rows, tile_cols, tile_count, send_rows, hub_ids,
):
    rows, _ = features.shape
    cols = out_bias.shape[0]
    hubs = hub_ids.shape[0]
    slots, halo = send_rows.shape[1:]
    chunk = 16
    n_chunk = cols // chunk
    z_ring = n_dom // Y_RING
    blocks = (rows + slots * halo + hubs) // BLK
    vmem = pl.BlockSpec(memory_space=pltpu.VMEM)
    dma = pltpu.SemaphoreType.DMA
    tiles = tile_values.shape[0]
    shape = jax.ShapeDtypeStruct
    carried = 2 * blocks * cols * BLK + 2 * tile_values.size + 4 * (8 + cols) * BLK
    extended, held_tiles, meta, bias = pl.pallas_call(
        functools.partial(exchange_kernel, n_dom, n_feat, cols, chunk),
        out_shape=(
            pltpu.VMEM((blocks, cols, BLK), BF16),
            pltpu.VMEM(tile_values.shape, BF16),
            pltpu.VMEM((8, BLK), I32),
            pltpu.VMEM((cols, BLK), F32),
        ),
        in_specs=[pl.BlockSpec(memory_space=pltpu.HBM)] * 9,
        out_specs=(vmem,) * 4,
        scratch_shapes=[
            pltpu.VMEM((features.shape[1], rows), BF16),
            pltpu.VMEM(weight.shape, BF16),
            pltpu.VMEM((slots, halo), I32),
            pltpu.VMEM((1, hubs), I32),
            pltpu.VMEM((slots, LO, halo), BF16),
            pltpu.VMEM((Y_RING * HUB_MOST, hubs), BF16),
            pltpu.VMEM((n_feat, n_chunk, chunk, rows), BF16),
            pltpu.VMEM((n_chunk, n_feat - 1, chunk, rows), BF16),
            pltpu.VMEM((n_chunk, slots, halo // BLK, chunk, BLK), BF16),
            pltpu.VMEM((n_feat, cols, BLK), BF16),
            pltpu.VMEM((n_feat - 1, cols, BLK), BF16),
            pltpu.VMEM((cols, BLK), BF16),
            pltpu.VMEM((Y_RING, cols, BLK), BF16),
            pltpu.VMEM((cols, Y_RING * HUB_MOST), BF16),
            pltpu.VMEM((z_ring, cols, Y_RING * HUB_MOST), BF16),
            pltpu.VMEM((2, 1, tiles), I32),
            pltpu.SMEM((1,), I32),
            pltpu.VMEM((1, cols), F32),
            dma((9,)),
            dma((n_chunk, n_feat - 1)),
            dma((n_chunk, n_feat - 1)),
            dma((n_chunk, slots)),
            dma((n_chunk, slots)),
            dma((n_feat - 1,)),
            dma((n_feat - 1,)),
            dma((Y_RING - 1,)),
            dma((Y_RING - 1,)),
            dma((z_ring - 1,)),
            dma((z_ring - 1,)),
            pltpu.SemaphoreType.REGULAR,
            pltpu.SemaphoreType.REGULAR,
            pltpu.SemaphoreType.REGULAR,
        ],
        compiler_params=pltpu.CompilerParams(
            collective_id=0,
            has_side_effects=True,
            vmem_limit_bytes=VMEM_MOST - carried - 65536,
        ),
        name="exchange",
    )(
        features.T, weight, send_rows[0], hub_ids[None, :], tile_values,
        tile_rows[None, :], tile_cols[None, :], tile_count, out_bias[None, :],
    )
    out_t = pl.pallas_call(
        tile_kernel,
        out_shape=shape((cols, rows), BF16),
        in_specs=[pl.BlockSpec(memory_space=pltpu.SMEM), vmem, vmem, vmem],
        out_specs=vmem,
        scratch_shapes=[pltpu.VMEM((rows // BLK + 1, cols, BLK), F32)],
        compiler_params=pltpu.CompilerParams(vmem_limit_bytes=16 * 2**20),
        name="tiles",
    )(meta, held_tiles, extended, bias)
    return out_t.T


def solution(mesh):
    in_specs = (
        P("dom", "feat"),
        P(),
        P("feat"),
        P("dom", None, None),
        P("dom"),
        P("dom"),
        P("dom"),
        P("dom", None, None),
        P(),
    )
    out_specs = P("dom", "feat")
    body = functools.partial(local, mesh.shape["dom"], mesh.shape["feat"])
    return jax.shard_map(body, mesh=mesh, in_specs=in_specs, out_specs=out_specs, check_vma=False)
```

time: 59.6 us -> 44.6 us (0.75)
  Pallas kernels: 54.4 us -> 43.9 us
  local copies, waits for them, and re-layouts: 4.23 us -> 0 us
    pallas_call x1, Pallas kernels: 46.3 us -> 38.5 us  [local(): pl.pallas_call(functools.partial(exchange_kernel, n_dom, n_feat, cols, ch...]
    unnamed x10 -> x0, local copies, waits for them, and re-layouts: 4.23 us -> none
    pallas_call x1, Pallas kernels: 8.05 us -> 5.35 us  [local(): pl.pallas_call(tile_kernel, out_shape=shape((cols, rows), BF16), in_specs...]
where the time goes in v2:
time: 44.6 us; the launch traced here: 44.5 us
  Pallas kernels  43.9 us (98%)
  between operations  0.66 us (1%)
    pallas_call x1, Pallas kernels, local(): pl.pallas_call(functools.partial(exchange_kernel, n_dom, n_feat, cols, ch...  38.5 us
    pallas_call x1, Pallas kernels, local(): pl.pallas_call(tile_kernel, out_shape=shape((cols, rows), BF16), in_specs...  5.35 us

profile of v2, /device:TPU:1, one launch (start us, length us, event | category | flops | bytes accessed | tf_op | source)
XLA Modules:
  0.0 44.5 jit_solution(4356934315021564672)
XLA Ops:
  0.7 38.5 %exchange.1 = (bf16[88,32,128]{2,1,0:T(8,128)(2,1)S(1)}, bf16[108,128,128]{2,1,0:T(8,128)(2,1)S(1)}, s32[8,128]{1,0:T(8,128)S(1)}, f32[32,128]{1,0:T(8,128)S(1)}) custom-call(bf16[76,2048]{1,0:T(8,128)(2,1)} %bitcast.7, bf16[608,256]{1,0:T(8,128)(2,1)} %w_hbm.1, s32[8,1024]{1,0:T(8,128)} %bitcast.8, s32[1,1024]{1,0:T(1,128)} %bitcast.9, ...), custom_call_target="tpu_custom_call" | custom-call | tf_op jit(solution)/shard_map/exchange/pallas_call | solution.py:387
  39.2 5.4 %tiles.1 = bf16[32,2048]{1,0:T(8,128)(2,1)} custom-call(s32[8,128]{1,0:T(8,128)S(1)} %get-tuple-element.9.meta_ref, bf16[108,128,128]{2,1,0:T(8,128)(2,1)S(1)} %get-tuple-element.10.tiles_ref, bf16[88,32,128]{2,1,0:T(8,128)(2,1)S(1)} %get-tuple-element.11.ext_ref, f32[32,128]{1,0:T(8,128)S(1)} %get-tuple-element.12.bias_ref), custom_call_target="tpu_custom_call" | custom-call | tf_op jit(solution)/shard_map/tiles/pallas_call | solution.py:441

commit v3 on v2

--- a/solution.py
+++ b/solution.py
@@ -288,6 +288,7 @@
                 y_copies[h, s].start()
 
     bulk(0)
+    bulk(1)
 
     for copy in hub_y:
         copy.wait()
@@ -326,7 +327,7 @@
         copy.start()
         hub_z.append(copy)
 
-    for h in range(1, n_chunk):
+    for h in range(2, n_chunk):
         bulk(h)
 
     for copy in hub_z:
@@ -351,14 +352,17 @@
 def tile_kernel(meta_ref, tiles_ref, ext_ref, bias_ref, out_ref, acc_ref):
     row_blocks = acc_ref.shape[0] - 1
     acc_ref[...] = jnp.zeros_like(acc_ref)
-    unroll = 6
+    unroll = 36
+    columns = ext_ref.shape[1]
 
     @pl.loop(0, tiles_ref.shape[0] // unroll)
     def _(step):
         products = []
-        for u in range(unroll):
+        for u in range(0, unroll, 2):
             t = step * unroll + u
-            products.append(dot(ext_ref[meta_ref[1, t]], tiles_ref[t], 1, 1))
+            left = jnp.concatenate([ext_ref[meta_ref[1, t]], ext_ref[meta_ref[1, t + 1]]], 0)
+            both = dot(left, tiles_ref[pl.ds(t, 2)].reshape(2 * BLK, BLK), 1, 1)
+            products += [both[:columns, :BLK], both[columns:, BLK:]]
         for u in range(unroll):
             acc_ref[meta_ref[0, step * unroll + u]] += products[u]
 
@@ -375,7 +379,7 @@
     cols = out_bias.shape[0]
     hubs = hub_ids.shape[0]
     slots, halo = send_rows.shape[1:]
-    chunk = 16
+    chunk = 8
     n_chunk = cols // chunk
     z_ring = n_dom // Y_RING
     blocks = (rows + slots * halo + hubs) // BLK

time: 44.6 us -> 41.3 us (0.926)
  Pallas kernels: 43.9 us -> 40.6 us
    pallas_call x1, Pallas kernels: 5.35 us -> 3 us  [local(): pl.pallas_call(tile_kernel, out_shape=shape((cols, rows), BF16), in_specs...]
    pallas_call x1, Pallas kernels: 38.5 us -> 37.6 us  [local(): pl.pallas_call(functools.partial(exchange_kernel, n_dom, n_feat, cols, ch...]
where the time goes in v3:
time: 41.3 us; the launch traced here: 41.2 us
  Pallas kernels  40.6 us (98%)
  between operations  0.66 us (2%)
    pallas_call x1, Pallas kernels, local(): pl.pallas_call(functools.partial(exchange_kernel, n_dom, n_feat, cols, ch...  37.6 us
    pallas_call x1, Pallas kernels, local(): pl.pallas_call(tile_kernel, out_shape=shape((cols, rows), BF16), in_specs...  3 us

profile of v3, /device:TPU:1, one launch (start us, length us, event | category | flops | bytes accessed | tf_op | source)
XLA Modules:
  0.0 41.2 jit_solution(7893359071752934887)
XLA Ops:
  0.7 37.6 %exchange.1 = (bf16[88,32,128]{2,1,0:T(8,128)(2,1)S(1)}, bf16[108,128,128]{2,1,0:T(8,128)(2,1)S(1)}, s32[8,128]{1,0:T(8,128)S(1)}, f32[32,128]{1,0:T(8,128)S(1)}) custom-call(bf16[76,2048]{1,0:T(8,128)(2,1)} %bitcast.7, bf16[608,256]{1,0:T(8,128)(2,1)} %w_hbm.1, s32[8,1024]{1,0:T(8,128)} %bitcast.8, s32[1,1024]{1,0:T(1,128)} %bitcast.9, ...), custom_call_target="tpu_custom_call" | custom-call | tf_op jit(solution)/shard_map/exchange/pallas_call | solution.py:391
  38.2 3.0 %tiles.1 = bf16[32,2048]{1,0:T(8,128)(2,1)} custom-call(s32[8,128]{1,0:T(8,128)S(1)} %get-tuple-element.9.meta_ref, bf16[108,128,128]{2,1,0:T(8,128)(2,1)S(1)} %get-tuple-element.10.tiles_ref, bf16[88,32,128]{2,1,0:T(8,128)(2,1)S(1)} %get-tuple-element.11.ext_ref, f32[32,128]{1,0:T(8,128)S(1)} %get-tuple-element.12.bias_ref), custom_call_target="tpu_custom_call" | custom-call | tf_op jit(solution)/shard_map/tiles/pallas_call | solution.py:445

commit v4 on v3

--- a/solution.py
+++ b/solution.py
@@ -31,12 +31,20 @@
     return jnp.where(mask, 1.0, 0.0).astype(BF16)
 
 
+def ascending(shape, swap=False):
+    a, b = lax.broadcasted_iota(I32, shape, 0), lax.broadcasted_iota(I32, shape, 1)
+    return b < a if swap else a < b
+
+
 def pick_groups(stacked, group_of, groups, height):
-    total = None
+    total = jnp.zeros((height, stacked.shape[1]), F32)
     for g in range(groups):
-        part = jnp.where(group_of == g, stacked[g * height : (g + 1) * height], 0.0)
-        total = part if total is None else total + part
+        total = jnp.where(group_of == g, stacked[g * height : (g + 1) * height], total)
     return total
+
+
+def as_row(x):
+    return jnp.concatenate([x[i : i + 1] for i in range(x.shape[0])], 1)
 
 
 def exchange_kernel(
@@ -96,21 +104,23 @@
         def _():
             tell(barrier, p, other)
 
-    loads[0].wait()
+    for i in range(3):
+        loads[i].wait()
+
     ids = hub_ref[...]
-    hubs = ids.shape[1]
-    owner = lax.div(ids, rows)
+    hubs = ids.size
+    f_in = w_ref.shape[0]
+    mine = lax.div(ids, rows) == p
+    mine_ones = ones_where(mine)
+    side = ids.shape[0]
+    in_row = dot(mine_ones, ones_where(ascending((BLK, BLK))))
+    above = jnp.sum(dot(ones_where(ascending((side, side), True)), mine_ones), 1, keepdims=True)
+    my_rank = (in_row + above).astype(I32)
     local_row = lax.rem(ids, rows)
-    owned = lax.broadcasted_iota(I32, (n_dom, hubs), 0) == owner
-    before = ones_where(
-        lax.broadcasted_iota(I32, (hubs, hubs), 0) < lax.broadcasted_iota(I32, (hubs, hubs), 1)
-    )
-    earlier = dot(ones_where(owned), before)
-    rank = jnp.sum(jnp.where(owned, earlier, 0.0), 0, keepdims=True).astype(I32)
-    place = lax.rem(rank + y * HUB_MOST, BLK)
-    taken = ones_where((lax.broadcasted_iota(I32, (BLK, hubs), 0) == place) & (owner == p))
+    place = as_row(jnp.where(mine, lax.rem(my_rank + y * HUB_MOST, BLK), -1))
+    taken = ones_where(lax.broadcasted_iota(I32, (BLK, hubs), 0) == place)
     halves = jnp.concatenate(
-        [lax.rem(local_row, LO).astype(F32), (lax.div(local_row, LO) + 1).astype(F32)]
+        [as_row(lax.rem(local_row, LO).astype(F32)), as_row((lax.div(local_row, LO) + 1).astype(F32))]
         + [jnp.zeros((14, hubs), F32)],
         0,
     ).astype(BF16)
@@ -118,8 +128,6 @@
     hub_row = (listed[0:1] + LO * (listed[1:2] - 1.0)).astype(I32)
     hub_pick = ones_where(lax.broadcasted_iota(I32, (rows, BLK), 0) == hub_row)
 
-    f_in = w_ref.shape[0]
-    loads[2].wait()
     pick = ones_where(
         lax.broadcasted_iota(I32, (BLK, f_in), 1)
         == lax.broadcasted_iota(I32, (BLK, f_in), 0) + j * k_in
@@ -127,12 +135,14 @@
     w_mine = dot(pick, w_ref[...])
     w_t = w_mine.T.astype(BF16)[:, :k_in]
 
-    loads[1].wait()
     ft = ft_ref[...]
     hub_ft = dot(ft, hub_pick).astype(BF16)
-    hub_part = dot(w_t, hub_ft).astype(BF16)
+    hub_part = dot(w_t, hub_ft)
+    half = cols // 2
     for d in range(n_feat):
-        hx_out[d] = hub_part[d * cols : (d + 1) * cols]
+        lower = hub_part[d * cols : d * cols + half]
+        upper = hub_part[d * cols + half : (d + 1) * cols]
+        hx_out[d] = (lower + pltpu.roll(upper, BLK // 2, 1)).astype(BF16)
 
     @pl.when(j < ring_desk)
     def _():
@@ -195,6 +205,37 @@
             )
             x_copies[h, d].start()
 
+    loads[3].wait()
+    for s in range(slots):
+        lo = lax.rem(send_ref[s : s + 1, :], LO)
+        hot_ref[s] = ones_where(lax.broadcasted_iota(I32, (LO, halo), 0) == lo)
+    packed = Y_RING * HUB_MOST
+    ids_row = as_row(ids)
+    owner = lax.div(ids_row, rows)
+    owned = lax.broadcasted_iota(I32, (n_dom, hubs), 0) == owner
+    earlier = dot(ones_where(owned), ones_where(ascending((hubs, hubs))))
+    rank = jnp.sum(jnp.where(owned, earlier, 0.0), 0, keepdims=True).astype(I32)
+    end_place = lax.rem(owner, Y_RING) * HUB_MOST + rank
+    end_z = lax.div(owner, Y_RING)
+    endhot_ref[...] = ones_where(lax.broadcasted_iota(I32, (packed, hubs), 0) == end_place)
+
+    for i in range(4, 8):
+        loads[i].wait()
+    tiles = meta_in.shape[2]
+    live = lax.broadcasted_iota(I32, (1, tiles), 1) < count_in[0]
+    meta_ref[0:1, 0:tiles] = jnp.where(live, meta_in[0], own_blocks)
+    meta_ref[1:2, 0:tiles] = meta_in[1]
+    eye = lax.broadcasted_iota(I32, (cols, cols), 0) == lax.broadcasted_iota(I32, (cols, cols), 1)
+    bias = jnp.sum(jnp.where(eye, bias_in[...], 0.0), 1, keepdims=True)
+    bias_ref[...] = jnp.broadcast_to(bias, (cols, BLK))
+
+    for s in range(slots):
+
+        @pl.when(jnp.logical_not(inside(-OFFSETS[s])))
+        def _():
+            first = own_blocks + s * slot_blocks
+            ext_ref[first : first + slot_blocks] = jnp.zeros((slot_blocks, cols, BLK), BF16)
+
     for copy in hub_x:
         copy.wait()
     hub_sum = hx_out[j].astype(F32)
@@ -228,32 +269,6 @@
         )
         copy.start()
         hub_y.append(copy)
-
-    loads[3].wait()
-    for s in range(slots):
-        lo = lax.rem(send_ref[s : s + 1, :], LO)
-        hot_ref[s] = ones_where(lax.broadcasted_iota(I32, (LO, halo), 0) == lo)
-    packed = Y_RING * HUB_MOST
-    end_place = lax.rem(owner, Y_RING) * HUB_MOST + rank
-    end_z = lax.div(owner, Y_RING)
-    endhot_ref[...] = ones_where(lax.broadcasted_iota(I32, (packed, hubs), 0) == end_place)
-
-    for i in range(4, 8):
-        loads[i].wait()
-    tiles = meta_in.shape[2]
-    live = lax.broadcasted_iota(I32, (1, tiles), 1) < count_in[0]
-    meta_ref[0:1, 0:tiles] = jnp.where(live, meta_in[0], own_blocks)
-    meta_ref[1:2, 0:tiles] = meta_in[1]
-    eye = lax.broadcasted_iota(I32, (cols, cols), 0) == lax.broadcasted_iota(I32, (cols, cols), 1)
-    bias = jnp.sum(jnp.where(eye, bias_in[...], 0.0), 1, keepdims=True)
-    bias_ref[...] = jnp.broadcast_to(bias, (cols, BLK))
-
-    for s in range(slots):
-
-        @pl.when(jnp.logical_not(inside(-OFFSETS[s])))
-        def _():
-            first = own_blocks + s * slot_blocks
-            ext_ref[first : first + slot_blocks] = jnp.zeros((slot_blocks, cols, BLK), BF16)
 
     y_copies = {}
 
@@ -288,19 +303,23 @@
                 y_copies[h, s].start()
 
     bulk(0)
-    bulk(1)
 
     for copy in hub_y:
         copy.wait()
+    arrived = [hy[source].astype(F32) for source in range(Y_RING)]
     for t in range(packed // BLK):
-        lane = lax.broadcasted_iota(I32, (cols, BLK), 1) + t * BLK
-        tile = jnp.zeros((cols, BLK), F32)
+        lane = lax.broadcasted_iota(I32, (half, BLK), 1) + t * BLK
+        low_tile = jnp.zeros((half, BLK), F32)
+        high_tile = jnp.zeros((half, BLK), F32)
         for source in range(Y_RING):
             low, high = source * HUB_MOST, (source + 1) * HUB_MOST
             if high <= t * BLK or low >= (t + 1) * BLK:
                 continue
-            tile = jnp.where((lane >= low) & (lane < high), hy[source].astype(F32), tile)
-        hpack[:, t * BLK : (t + 1) * BLK] = tile.astype(BF16)
+            here = (lane >= low) & (lane < high)
+            low_tile = jnp.where(here, arrived[source], low_tile)
+            high_tile = jnp.where(here, pltpu.roll(arrived[source], BLK // 2, 1), high_tile)
+        hpack[:half, t * BLK : (t + 1) * BLK] = low_tile.astype(BF16)
+        hpack[half:, t * BLK : (t + 1) * BLK] = high_tile.astype(BF16)
     hz[z] = hpack[...]
 
     @pl.when(j == ring_desk)
@@ -327,7 +346,7 @@
         copy.start()
         hub_z.append(copy)
 
-    for h in range(2, n_chunk):
+    for h in range(1, n_chunk):
         bulk(h)
 
     for copy in hub_z:
@@ -402,16 +421,16 @@
             pltpu.VMEM((features.shape[1], rows), BF16),
             pltpu.VMEM(weight.shape, BF16),
             pltpu.VMEM((slots, halo), I32),
-            pltpu.VMEM((1, hubs), I32),
+            pltpu.VMEM((hubs // BLK, BLK), I32),
             pltpu.VMEM((slots, LO, halo), BF16),
             pltpu.VMEM((Y_RING * HUB_MOST, hubs), BF16),
             pltpu.VMEM((n_feat, n_chunk, chunk, rows), BF16),
             pltpu.VMEM((n_chunk, n_feat - 1, chunk, rows), BF16),
             pltpu.VMEM((n_chunk, slots, halo // BLK, chunk, BLK), BF16),
-            pltpu.VMEM((n_feat, cols, BLK), BF16),
-            pltpu.VMEM((n_feat - 1, cols, BLK), BF16),
-            pltpu.VMEM((cols, BLK), BF16),
-            pltpu.VMEM((Y_RING, cols, BLK), BF16),
+            pltpu.VMEM((n_feat, cols // 2, BLK), BF16),
+            pltpu.VMEM((n_feat - 1, cols // 2, BLK), BF16),
+            pltpu.VMEM((cols // 2, BLK), BF16),
+            pltpu.VMEM((Y_RING, cols // 2, BLK), BF16),
             pltpu.VMEM((cols, Y_RING * HUB_MOST), BF16),
             pltpu.VMEM((z_ring, cols, Y_RING * HUB_MOST), BF16),
             pltpu.VMEM((2, 1, tiles), I32),
@@ -439,7 +458,7 @@
         ),
         name="exchange",
     )(
-        features.T, weight, send_rows[0], hub_ids[None, :], tile_values,
+        features.T, weight, send_rows[0], hub_ids.reshape(hubs // BLK, BLK), tile_values,
         tile_rows[None, :], tile_cols[None, :], tile_count, out_bias[None, :],
     )
     out_t = pl.pallas_call(

time: 41.3 us -> 39.5 us (0.956); the launches traced: 41.2 us -> 38.9 us
  Pallas kernels: 40.6 us -> 38.2 us
    pallas_call x1, Pallas kernels: 37.6 us -> 35.2 us  [local(): pl.pallas_call(functools.partial(exchange_kernel, n_dom, n_feat, cols, ch...]
where the time goes in v4:
time: 39.5 us; the launch traced here: 38.9 us
  Pallas kernels  38.2 us (97%)
  between operations  0.66 us (2%)
    pallas_call x1, Pallas kernels, local(): pl.pallas_call(functools.partial(exchange_kernel, n_dom, n_feat, cols, ch...  35.2 us
    pallas_call x1, Pallas kernels, local(): pl.pallas_call(tile_kernel, out_shape=shape((cols, rows), BF16), in_specs...  3.03 us

profile of v4, /device:TPU:1, one launch (start us, length us, event | category | flops | bytes accessed | tf_op | source)
XLA Modules:
  0.0 38.9 jit_solution(12700695364383159440)
XLA Ops:
  0.7 35.2 %exchange.1 = (bf16[88,32,128]{2,1,0:T(8,128)(2,1)S(1)}, bf16[108,128,128]{2,1,0:T(8,128)(2,1)S(1)}, s32[8,128]{1,0:T(8,128)S(1)}, f32[32,128]{1,0:T(8,128)S(1)}) custom-call(bf16[76,2048]{1,0:T(8,128)(2,1)} %bitcast.7, bf16[608,256]{1,0:T(8,128)(2,1)} %w_hbm.1, s32[8,1024]{1,0:T(8,128)} %bitcast.8, s32[8,128]{1,0:T(8,128)} %bitcast.9, ...), custom_call_target="tpu_custom_call" | custom-call | tf_op jit(solution)/shard_map/exchange/pallas_call | solution.py:410
  35.8 3.0 %tiles.1 = bf16[32,2048]{1,0:T(8,128)(2,1)} custom-call(s32[8,128]{1,0:T(8,128)S(1)} %get-tuple-element.9.meta_ref, bf16[108,128,128]{2,1,0:T(8,128)(2,1)S(1)} %get-tuple-element.10.tiles_ref, bf16[88,32,128]{2,1,0:T(8,128)(2,1)S(1)} %get-tuple-element.11.ext_ref, f32[32,128]{1,0:T(8,128)S(1)} %get-tuple-element.12.bias_ref), custom_call_target="tpu_custom_call" | custom-call | tf_op jit(solution)/shard_map/tiles/pallas_call | solution.py:464

commit v5 on v4

--- a/solution.py
+++ b/solution.py
@@ -41,6 +41,10 @@
     for g in range(groups):
         total = jnp.where(group_of == g, stacked[g * height : (g + 1) * height], total)
     return total
+
+
+def arrived_in(ref, sem):
+    pltpu.make_async_copy(ref, ref, sem).wait()
 
 
 def as_row(x):
@@ -104,12 +108,10 @@
         def _():
             tell(barrier, p, other)
 
-    for i in range(3):
-        loads[i].wait()
+    loads[0].wait()
 
     ids = hub_ref[...]
     hubs = ids.size
-    f_in = w_ref.shape[0]
     mine = lax.div(ids, rows) == p
     mine_ones = ones_where(mine)
     side = ids.shape[0]
@@ -128,6 +130,8 @@
     hub_row = (listed[0:1] + LO * (listed[1:2] - 1.0)).astype(I32)
     hub_pick = ones_where(lax.broadcasted_iota(I32, (rows, BLK), 0) == hub_row)
 
+    f_in = w_ref.shape[0]
+    loads[2].wait()
     pick = ones_where(
         lax.broadcasted_iota(I32, (BLK, f_in), 1)
         == lax.broadcasted_iota(I32, (BLK, f_in), 0) + j * k_in
@@ -135,6 +139,7 @@
     w_mine = dot(pick, w_ref[...])
     w_t = w_mine.T.astype(BF16)[:, :k_in]
 
+    loads[1].wait()
     ft = ft_ref[...]
     hub_ft = dot(ft, hub_pick).astype(BF16)
     hub_part = dot(w_t, hub_ft)
@@ -173,20 +178,17 @@
         for d in range(1, z_ring):
             tell(barrier, z_at(d), ring_desk)
 
-    hub_x = []
     for d in range(1, n_feat):
         copy = pltpu.make_async_remote_copy(
             src_ref=hx_out.at[feat_at(d)],
             dst_ref=hx.at[d - 1],
-            send_sem=hxs.at[d - 1],
-            recv_sem=hxr.at[d - 1],
+            send_sem=hxs,
+            recv_sem=hxr,
             device_id={"feat": feat_at(d)},
             device_id_type=MESH,
         )
         copy.start()
-        hub_x.append(copy)
-
-    x_copies = {}
+
     for h in range(n_chunk):
         left = jnp.concatenate(
             [w_t[d * cols + h * chunk : d * cols + (h + 1) * chunk] for d in range(n_feat)], 0
@@ -195,15 +197,15 @@
         for d in range(n_feat):
             sx[d, h] = part[d * chunk : (d + 1) * chunk]
         for d in range(1, n_feat):
-            x_copies[h, d] = pltpu.make_async_remote_copy(
+            copy = pltpu.make_async_remote_copy(
                 src_ref=sx.at[feat_at(d), h],
                 dst_ref=rx.at[h, d - 1],
-                send_sem=sxs.at[h, d - 1],
-                recv_sem=sxr.at[h, d - 1],
+                send_sem=sxs,
+                recv_sem=sxr.at[h],
                 device_id={"feat": feat_at(d)},
                 device_id_type=MESH,
             )
-            x_copies[h, d].start()
+            copy.start()
 
     loads[3].wait()
     for s in range(slots):
@@ -236,8 +238,7 @@
             first = own_blocks + s * slot_blocks
             ext_ref[first : first + slot_blocks] = jnp.zeros((slot_blocks, cols, BLK), BF16)
 
-    for copy in hub_x:
-        copy.wait()
+    arrived_in(hx, hxr)
     hub_sum = hx_out[j].astype(F32)
     for d in range(1, n_feat):
         hub_sum = hub_sum + hx[d - 1].astype(F32)
@@ -257,25 +258,20 @@
     def _():
         pl.semaphore_wait(near_in, 1)
 
-    hub_y = []
     for d in range(1, Y_RING):
         copy = pltpu.make_async_remote_copy(
             src_ref=hub_out,
             dst_ref=hy.at[y],
-            send_sem=hys.at[d - 1],
-            recv_sem=hyr.at[d - 1],
+            send_sem=hys,
+            recv_sem=hyr,
             device_id={"dom": y_at(d)},
             device_id_type=MESH,
         )
         copy.start()
-        hub_y.append(copy)
-
-    y_copies = {}
 
     def bulk(h):
         span = slice(h * chunk, (h + 1) * chunk)
-        for d in range(1, n_feat):
-            x_copies[h, d].wait()
+        arrived_in(rx.at[h], sxr.at[h])
         total = sx[j, h].astype(F32)
         for d in range(1, n_feat):
             total = total + rx[h, d - 1].astype(F32)
@@ -289,23 +285,23 @@
             for b in range(slot_blocks):
                 sy[h, s, b] = rows_out[:, b * BLK : (b + 1) * BLK]
             first = own_blocks + s * slot_blocks
-            y_copies[h, s] = pltpu.make_async_remote_copy(
+            copy = pltpu.make_async_remote_copy(
                 src_ref=sy.at[h, s],
                 dst_ref=ext_ref.at[first : first + slot_blocks, span, :],
-                send_sem=sys_.at[h, s],
-                recv_sem=syr.at[h, s],
+                send_sem=sys_.at[s],
+                recv_sem=syr.at[s],
                 device_id={"dom": p + OFFSETS[s]},
                 device_id_type=MESH,
             )
 
             @pl.when(inside(OFFSETS[s]))
             def _():
-                y_copies[h, s].start()
+                copy.start()
 
     bulk(0)
-
-    for copy in hub_y:
-        copy.wait()
+    bulk(1)
+
+    arrived_in(hy.at[0 : Y_RING - 1], hyr)
     arrived = [hy[source].astype(F32) for source in range(Y_RING)]
     for t in range(packed // BLK):
         lane = lax.broadcasted_iota(I32, (half, BLK), 1) + t * BLK
@@ -333,39 +329,43 @@
     def _():
         pl.semaphore_wait(ring_in, 1)
 
-    hub_z = []
     for d in range(1, z_ring):
         copy = pltpu.make_async_remote_copy(
             src_ref=hpack,
             dst_ref=hz.at[z],
-            send_sem=hzs.at[d - 1],
-            recv_sem=hzr.at[d - 1],
+            send_sem=hzs,
+            recv_sem=hzr,
             device_id={"dom": z_at(d)},
             device_id_type=MESH,
         )
         copy.start()
-        hub_z.append(copy)
-
-    for h in range(1, n_chunk):
+
+    for h in range(2, n_chunk):
         bulk(h)
 
-    for copy in hub_z:
-        copy.wait()
+    arrived_in(hz.at[0 : z_ring - 1], hzr)
     everyone = jnp.concatenate([hz[source] for source in range(z_ring)], 0)
     hub_block = pick_groups(dot(everyone, endhot_ref[...]), end_z, z_ring, cols).astype(BF16)
     for b in range(hubs // BLK):
         ext_ref[hub_first + b] = hub_block[:, b * BLK : (b + 1) * BLK]
 
     loads[8].wait()
-    for (h, s), copy in y_copies.items():
+    for s in range(slots):
+        first = own_blocks + s * slot_blocks
+        slot_rows = ext_ref.at[first : first + slot_blocks]
+
+        @pl.when(inside(-OFFSETS[s]))
+        def _():
+            arrived_in(slot_rows, syr.at[s])
 
         @pl.when(inside(OFFSETS[s]))
         def _():
-            copy.wait_send()
-
-        @pl.when(inside(-OFFSETS[s]))
-        def _():
-            copy.wait_recv()
+            arrived_in(slot_rows, sys_.at[s])
+
+    arrived_in(hx, hxs)
+    arrived_in(rx, sxs)
+    arrived_in(hy.at[0 : Y_RING - 1], hys)
+    arrived_in(hz.at[0 : z_ring - 1], hzs)
 
 
 def tile_kernel(meta_ref, tiles_ref, ext_ref, bias_ref, out_ref, acc_ref):
@@ -437,16 +437,16 @@
             pltpu.SMEM((1,), I32),
             pltpu.VMEM((1, cols), F32),
             dma((9,)),
-            dma((n_chunk, n_feat - 1)),
-            dma((n_chunk, n_feat - 1)),
-            dma((n_chunk, slots)),
-            dma((n_chunk, slots)),
-            dma((n_feat - 1,)),
-            dma((n_feat - 1,)),
-            dma((Y_RING - 1,)),
-            dma((Y_RING - 1,)),
-            dma((z_ring - 1,)),
-            dma((z_ring - 1,)),
+            dma,
+            dma((n_chunk,)),
+            dma((slots,)),
+            dma((slots,)),
+            dma,
+            dma,
+            dma,
+            dma,
+            dma,
+            dma,
             pltpu.SemaphoreType.REGULAR,
             pltpu.SemaphoreType.REGULAR,
             pltpu.SemaphoreType.REGULAR,

time: 39.5 us -> 38.2 us (0.967); the launches traced: 38.9 us -> 38.1 us
  Pallas kernels: 38.2 us -> 37.4 us
    pallas_call x1, Pallas kernels: 35.2 us -> 34.4 us  [local(): pl.pallas_call(functools.partial(exchange_kernel, n_dom, n_feat, cols, ch...]
where the time goes in v5:
time: 38.2 us; the launch traced here: 38.1 us
  Pallas kernels  37.4 us (98%)
  between operations  0.66 us (2%)
    pallas_call x1, Pallas kernels, local(): pl.pallas_call(functools.partial(exchange_kernel, n_dom, n_feat, cols, ch...  34.4 us
    pallas_call x1, Pallas kernels, local(): pl.pallas_call(tile_kernel, out_shape=shape((cols, rows), BF16), in_specs...  3.04 us

profile of v5, /device:TPU:1, one launch (start us, length us, event | category | flops | bytes accessed | tf_op | source)
XLA Modules:
  0.0 38.1 jit_solution(15427973516280559793)
XLA Ops:
  0.7 34.4 %exchange.1 = (bf16[88,32,128]{2,1,0:T(8,128)(2,1)S(1)}, bf16[108,128,128]{2,1,0:T(8,128)(2,1)S(1)}, s32[8,128]{1,0:T(8,128)S(1)}, f32[32,128]{1,0:T(8,128)S(1)}) custom-call(bf16[76,2048]{1,0:T(8,128)(2,1)} %bitcast.7, bf16[608,256]{1,0:T(8,128)(2,1)} %w_hbm.1, s32[8,1024]{1,0:T(8,128)} %bitcast.8, s32[8,128]{1,0:T(8,128)} %bitcast.9, ...), custom_call_target="tpu_custom_call" | custom-call | tf_op jit(solution)/shard_map/exchange/pallas_call | solution.py:410
  35.0 3.0 %tiles.1 = bf16[32,2048]{1,0:T(8,128)(2,1)} custom-call(s32[8,128]{1,0:T(8,128)S(1)} %get-tuple-element.9.meta_ref, bf16[108,128,128]{2,1,0:T(8,128)(2,1)S(1)} %get-tuple-element.10.tiles_ref, bf16[88,32,128]{2,1,0:T(8,128)(2,1)S(1)} %get-tuple-element.11.ext_ref, f32[32,128]{1,0:T(8,128)S(1)} %get-tuple-element.12.bias_ref), custom_call_target="tpu_custom_call" | custom-call | tf_op jit(solution)/shard_map/tiles/pallas_call | solution.py:464

commit v6 on v5

--- a/solution.py
+++ b/solution.py
@@ -54,9 +54,9 @@
 def exchange_kernel(
     n_dom, n_feat, cols, chunk,
     ft_hbm, w_hbm, send_hbm, hub_hbm, tiles_hbm, rows_hbm, cols_hbm, count_hbm, bias_hbm,
-    ext_ref, tiles_ref, meta_ref, bias_ref,
+    ext_ref, tiles_ref, meta_smem, bias_ref,
     ft_ref, w_ref, send_ref, hub_ref, hot_ref, endhot_ref, sx, rx, sy,
-    hx_out, hx, hub_out, hy, hpack, hz, meta_in, count_in, bias_in,
+    hx_out, hx, hub_out, hy, hpack, hz, meta_in, meta_ref, count_in, bias_in,
     in_sem, sxs, sxr, sys_, syr, hxs, hxr, hys, hyr, hzs, hzr, feat_in, near_in, ring_in,
 ):
     p = lax.axis_index("dom")
@@ -71,7 +71,9 @@
     own_blocks = rows // BLK
     slot_blocks = halo // BLK
     hub_first = own_blocks + slots * slot_blocks
-    near_desk, ring_desk = n_feat - 1, n_feat - 2
+    near_desk, ring_desk = n_feat - 1, n_feat - 3
+    desks = (near_desk, ring_desk)
+    at_desk = (j == near_desk) | (j == ring_desk)
 
     loads = []
     for i, (src, dst) in enumerate(
@@ -102,7 +104,9 @@
         return (p + o >= 0) & (p + o < n_dom)
 
     barrier = pltpu.get_barrier_semaphore()
-    for other in range(ring_desk):
+    for other in range(n_feat):
+        if other in desks:
+            continue
 
         @pl.when(j != other)
         def _():
@@ -149,16 +153,17 @@
         upper = hub_part[d * cols + half : (d + 1) * cols]
         hx_out[d] = (lower + pltpu.roll(upper, BLK // 2, 1)).astype(BF16)
 
-    @pl.when(j < ring_desk)
+    @pl.when(jnp.logical_not(at_desk))
     def _():
         pl.semaphore_wait(barrier, n_feat - 1)
 
-    @pl.when(j == 0)
-    def _():
-        tell(feat_in, p, near_desk)
-        tell(feat_in, p, ring_desk)
-
-    @pl.when(j >= ring_desk)
+    for desk in desks:
+
+        @pl.when(j == desk - 1)
+        def _():
+            tell(feat_in, p, desk)
+
+    @pl.when(at_desk)
     def _():
         pl.semaphore_wait(feat_in, 1)
 
@@ -227,6 +232,8 @@
     live = lax.broadcasted_iota(I32, (1, tiles), 1) < count_in[0]
     meta_ref[0:1, 0:tiles] = jnp.where(live, meta_in[0], own_blocks)
     meta_ref[1:2, 0:tiles] = meta_in[1]
+    hand_over = pltpu.make_async_copy(meta_ref, meta_smem, in_sem.at[4])
+    hand_over.start()
     eye = lax.broadcasted_iota(I32, (cols, cols), 0) == lax.broadcasted_iota(I32, (cols, cols), 1)
     bias = jnp.sum(jnp.where(eye, bias_in[...], 0.0), 1, keepdims=True)
     bias_ref[...] = jnp.broadcast_to(bias, (cols, BLK))
@@ -237,6 +244,14 @@
         def _():
             first = own_blocks + s * slot_blocks
             ext_ref[first : first + slot_blocks] = jnp.zeros((slot_blocks, cols, BLK), BF16)
+
+    @pl.when(j == near_desk)
+    def _():
+        before_p = lax.min(p, REACH)
+        after_p = lax.min(n_dom - 1 - p, REACH)
+        pl.semaphore_wait(barrier, before_p + after_p + Y_RING - 1)
+        for other in range(n_feat - 1):
+            tell(near_in, p, other)
 
     arrived_in(hx, hxr)
     hub_sum = hx_out[j].astype(F32)
@@ -245,14 +260,6 @@
     hub_mine = hub_sum.astype(BF16)
     hub_out[...] = hub_mine
     hy[y] = hub_mine
-
-    @pl.when(j == near_desk)
-    def _():
-        before_p = lax.min(p, REACH)
-        after_p = lax.min(n_dom - 1 - p, REACH)
-        pl.semaphore_wait(barrier, before_p + after_p + Y_RING - 1)
-        for other in range(n_feat - 1):
-            tell(near_in, p, other)
 
     @pl.when(j != near_desk)
     def _():
@@ -350,6 +357,7 @@
         ext_ref[hub_first + b] = hub_block[:, b * BLK : (b + 1) * BLK]
 
     loads[8].wait()
+    hand_over.wait()
     for s in range(slots):
         first = own_blocks + s * slot_blocks
         slot_rows = ext_ref.at[first : first + slot_blocks]
@@ -412,11 +420,11 @@
         out_shape=(
             pltpu.VMEM((blocks, cols, BLK), BF16),
             pltpu.VMEM(tile_values.shape, BF16),
-            pltpu.VMEM((8, BLK), I32),
+            pltpu.SMEM((8, BLK), I32),
             pltpu.VMEM((cols, BLK), F32),
         ),
         in_specs=[pl.BlockSpec(memory_space=pltpu.HBM)] * 9,
-        out_specs=(vmem,) * 4,
+        out_specs=(vmem, vmem, pl.BlockSpec(memory_space=pltpu.SMEM), vmem),
         scratch_shapes=[
             pltpu.VMEM((features.shape[1], rows), BF16),
             pltpu.VMEM(weight.shape, BF16),
@@ -434,6 +442,7 @@
             pltpu.VMEM((cols, Y_RING * HUB_MOST), BF16),
             pltpu.VMEM((z_ring, cols, Y_RING * HUB_MOST), BF16),
             pltpu.VMEM((2, 1, tiles), I32),
+            pltpu.VMEM((8, BLK), I32),
             pltpu.SMEM((1,), I32),
             pltpu.VMEM((1, cols), F32),
             dma((9,)),

time: 38.2 us -> 38.5 us (level)
  Pallas kernels: 37.4 us -> 37.8 us
    pallas_call x1, Pallas kernels: 34.4 us -> 35.3 us  [local(): pl.pallas_call(functools.partial(exchange_kernel, n_dom, n_feat, cols, ch...]
    pallas_call x1, Pallas kernels: 3.04 us -> 2.43 us  [local(): pl.pallas_call(tile_kernel, out_shape=shape((cols, rows), BF16), in_specs...]
where the time goes in v6:
time: 38.5 us; the launch traced here: 38.4 us
  Pallas kernels  37.8 us (98%)
  between operations  0.66 us (2%)
    pallas_call x1, Pallas kernels, local(): pl.pallas_call(functools.partial(exchange_kernel, n_dom, n_feat, cols, ch...  35.3 us
    pallas_call x1, Pallas kernels, local(): pl.pallas_call(tile_kernel, out_shape=shape((cols, rows), BF16), in_specs...  2.43 us

profile of v6, /device:TPU:1, one launch (start us, length us, event | category | flops | bytes accessed | tf_op | source)
XLA Modules:
  0.0 38.4 jit_solution(16379503636228072962)
XLA Ops:
  0.7 35.3 %exchange.1 = (bf16[88,32,128]{2,1,0:T(8,128)(2,1)S(1)}, bf16[108,128,128]{2,1,0:T(8,128)(2,1)S(1)}, s32[8,128]{1,0:T(8,128)S(4)}, f32[32,128]{1,0:T(8,128)S(1)}) custom-call(bf16[76,2048]{1,0:T(8,128)(2,1)} %bitcast.7, bf16[608,256]{1,0:T(8,128)(2,1)} %w_hbm.1, s32[8,1024]{1,0:T(8,128)} %bitcast.8, s32[8,128]{1,0:T(8,128)} %bitcast.9, ...), custom_call_target="tpu_custom_call" | custom-call | tf_op jit(solution)/shard_map/exchange/pallas_call | solution.py:418
  36.0 2.4 %tiles.1 = bf16[32,2048]{1,0:T(8,128)(2,1)} custom-call(s32[8,128]{1,0:T(8,128)S(4)} %get-tuple-element.9.meta_ref, bf16[108,128,128]{2,1,0:T(8,128)(2,1)S(1)} %get-tuple-element.10.tiles_ref, bf16[88,32,128]{2,1,0:T(8,128)(2,1)S(1)} %get-tuple-element.11.ext_ref, f32[32,128]{1,0:T(8,128)S(1)} %get-tuple-element.12.bias_ref), custom_call_target="tpu_custom_call" | custom-call | tf_op jit(solution)/shard_map/tiles/pallas_call | solution.py:473

commit v7 on v6

--- a/solution.py
+++ b/solution.py
@@ -45,6 +45,10 @@
 
 def arrived_in(ref, sem):
     pltpu.make_async_copy(ref, ref, sem).wait()
+
+
+def far_first(ring):
+    return sorted(range(1, ring), key=lambda d: -min(d, ring - d))
 
 
 def as_row(x):
@@ -183,7 +187,7 @@
         for d in range(1, z_ring):
             tell(barrier, z_at(d), ring_desk)
 
-    for d in range(1, n_feat):
+    for d in far_first(n_feat):
         copy = pltpu.make_async_remote_copy(
             src_ref=hx_out.at[feat_at(d)],
             dst_ref=hx.at[d - 1],
@@ -201,7 +205,7 @@
         part = dot(left, ft).astype(BF16)
         for d in range(n_feat):
             sx[d, h] = part[d * chunk : (d + 1) * chunk]
-        for d in range(1, n_feat):
+        for d in far_first(n_feat):
             copy = pltpu.make_async_remote_copy(
                 src_ref=sx.at[feat_at(d), h],
                 dst_ref=rx.at[h, d - 1],
@@ -265,7 +269,7 @@
     def _():
         pl.semaphore_wait(near_in, 1)
 
-    for d in range(1, Y_RING):
+    for d in far_first(Y_RING):
         copy = pltpu.make_async_remote_copy(
             src_ref=hub_out,
             dst_ref=hy.at[y],
@@ -306,6 +310,14 @@
                 copy.start()
 
     bulk(0)
+
+    @pl.when(j == ring_desk)
+    def _():
+        pl.semaphore_wait(barrier, z_ring - 1)
+        for other in range(n_feat):
+            if other != ring_desk:
+                tell(ring_in, p, other)
+
     bulk(1)
 
     arrived_in(hy.at[0 : Y_RING - 1], hyr)
@@ -325,18 +337,11 @@
         hpack[half:, t * BLK : (t + 1) * BLK] = high_tile.astype(BF16)
     hz[z] = hpack[...]
 
-    @pl.when(j == ring_desk)
-    def _():
-        pl.semaphore_wait(barrier, z_ring - 1)
-        for other in range(n_feat):
-            if other != ring_desk:
-                tell(ring_in, p, other)
-
     @pl.when(j != ring_desk)
     def _():
         pl.semaphore_wait(ring_in, 1)
 
-    for d in range(1, z_ring):
+    for d in far_first(z_ring):
         copy = pltpu.make_async_remote_copy(
             src_ref=hpack,
             dst_ref=hz.at[z],

time: 38.5 us -> 35.1 us (0.912)
  Pallas kernels: 37.8 us -> 34.2 us
    pallas_call x1, Pallas kernels: 35.3 us -> 31.8 us  [local(): pl.pallas_call(functools.partial(exchange_kernel, n_dom, n_feat, cols, ch...]
where the time goes in v7:
time: 35.1 us; the launch traced here: 34.9 us
  Pallas kernels  34.2 us (97%)
  between operations  0.66 us (2%)
    pallas_call x1, Pallas kernels, local(): pl.pallas_call(functools.partial(exchange_kernel, n_dom, n_feat, cols, ch...  31.8 us
    pallas_call x1, Pallas kernels, local(): pl.pallas_call(tile_kernel, out_shape=shape((cols, rows), BF16), in_specs...  2.43 us

profile of v7, /device:TPU:1, one launch (start us, length us, event | category | flops | bytes accessed | tf_op | source)
XLA Modules:
  0.0 34.9 jit_solution(4182096958206860284)
XLA Ops:
  0.7 31.8 %exchange.1 = (bf16[88,32,128]{2,1,0:T(8,128)(2,1)S(1)}, bf16[108,128,128]{2,1,0:T(8,128)(2,1)S(1)}, s32[8,128]{1,0:T(8,128)S(4)}, f32[32,128]{1,0:T(8,128)S(1)}) custom-call(bf16[76,2048]{1,0:T(8,128)(2,1)} %bitcast.7, bf16[608,256]{1,0:T(8,128)(2,1)} %w_hbm.1, s32[8,1024]{1,0:T(8,128)} %bitcast.8, s32[8,128]{1,0:T(8,128)} %bitcast.9, ...), custom_call_target="tpu_custom_call" | custom-call | tf_op jit(solution)/shard_map/exchange/pallas_call | solution.py:423
  32.5 2.4 %tiles.1 = bf16[32,2048]{1,0:T(8,128)(2,1)} custom-call(s32[8,128]{1,0:T(8,128)S(4)} %get-tuple-element.9.meta_ref, bf16[108,128,128]{2,1,0:T(8,128)(2,1)S(1)} %get-tuple-element.10.tiles_ref, bf16[88,32,128]{2,1,0:T(8,128)(2,1)S(1)} %get-tuple-element.11.ext_ref, f32[32,128]{1,0:T(8,128)S(1)} %get-tuple-element.12.bias_ref), custom_call_target="tpu_custom_call" | custom-call | tf_op jit(solution)/shard_map/tiles/pallas_call | solution.py:478

commit v8 on v7

--- a/solution.py
+++ b/solution.py
@@ -220,35 +220,6 @@
     for s in range(slots):
         lo = lax.rem(send_ref[s : s + 1, :], LO)
         hot_ref[s] = ones_where(lax.broadcasted_iota(I32, (LO, halo), 0) == lo)
-    packed = Y_RING * HUB_MOST
-    ids_row = as_row(ids)
-    owner = lax.div(ids_row, rows)
-    owned = lax.broadcasted_iota(I32, (n_dom, hubs), 0) == owner
-    earlier = dot(ones_where(owned), ones_where(ascending((hubs, hubs))))
-    rank = jnp.sum(jnp.where(owned, earlier, 0.0), 0, keepdims=True).astype(I32)
-    end_place = lax.rem(owner, Y_RING) * HUB_MOST + rank
-    end_z = lax.div(owner, Y_RING)
-    endhot_ref[...] = ones_where(lax.broadcasted_iota(I32, (packed, hubs), 0) == end_place)
-
-    for i in range(4, 8):
-        loads[i].wait()
-    tiles = meta_in.shape[2]
-    live = lax.broadcasted_iota(I32, (1, tiles), 1) < count_in[0]
-    meta_ref[0:1, 0:tiles] = jnp.where(live, meta_in[0], own_blocks)
-    meta_ref[1:2, 0:tiles] = meta_in[1]
-    hand_over = pltpu.make_async_copy(meta_ref, meta_smem, in_sem.at[4])
-    hand_over.start()
-    eye = lax.broadcasted_iota(I32, (cols, cols), 0) == lax.broadcasted_iota(I32, (cols, cols), 1)
-    bias = jnp.sum(jnp.where(eye, bias_in[...], 0.0), 1, keepdims=True)
-    bias_ref[...] = jnp.broadcast_to(bias, (cols, BLK))
-
-    for s in range(slots):
-
-        @pl.when(jnp.logical_not(inside(-OFFSETS[s])))
-        def _():
-            first = own_blocks + s * slot_blocks
-            ext_ref[first : first + slot_blocks] = jnp.zeros((slot_blocks, cols, BLK), BF16)
-
     @pl.when(j == near_desk)
     def _():
         before_p = lax.min(p, REACH)
@@ -279,6 +250,8 @@
             device_id_type=MESH,
         )
         copy.start()
+
+    packed = Y_RING * HUB_MOST
 
     def bulk(h):
         span = slice(h * chunk, (h + 1) * chunk)
@@ -355,6 +328,34 @@
     for h in range(2, n_chunk):
         bulk(h)
 
+    ids_row = as_row(ids)
+    owner = lax.div(ids_row, rows)
+    owned = lax.broadcasted_iota(I32, (n_dom, hubs), 0) == owner
+    earlier = dot(ones_where(owned), ones_where(ascending((hubs, hubs))))
+    rank = jnp.sum(jnp.where(owned, earlier, 0.0), 0, keepdims=True).astype(I32)
+    end_place = lax.rem(owner, Y_RING) * HUB_MOST + rank
+    end_z = lax.div(owner, Y_RING)
+    endhot_ref[...] = ones_where(lax.broadcasted_iota(I32, (packed, hubs), 0) == end_place)
+
+    for i in range(4, 8):
+        loads[i].wait()
+    tiles = meta_in.shape[2]
+    live = lax.broadcasted_iota(I32, (1, tiles), 1) < count_in[0]
+    meta_ref[0:1, 0:tiles] = jnp.where(live, meta_in[0], own_blocks)
+    meta_ref[1:2, 0:tiles] = meta_in[1]
+    hand_over = pltpu.make_async_copy(meta_ref, meta_smem, in_sem.at[4])
+    hand_over.start()
+    eye = lax.broadcasted_iota(I32, (cols, cols), 0) == lax.broadcasted_iota(I32, (cols, cols), 1)
+    bias = jnp.sum(jnp.where(eye, bias_in[...], 0.0), 1, keepdims=True)
+    bias_ref[...] = jnp.broadcast_to(bias, (cols, BLK))
+
+    for s in range(slots):
+
+        @pl.when(jnp.logical_not(inside(-OFFSETS[s])))
+        def _():
+            first = own_blocks + s * slot_blocks
+            ext_ref[first : first + slot_blocks] = jnp.zeros((slot_blocks, cols, BLK), BF16)
+
     arrived_in(hz.at[0 : z_ring - 1], hzr)
     everyone = jnp.concatenate([hz[source] for source in range(z_ring)], 0)
     hub_block = pick_groups(dot(everyone, endhot_ref[...]), end_z, z_ring, cols).astype(BF16)
@@ -384,7 +385,7 @@
 def tile_kernel(meta_ref, tiles_ref, ext_ref, bias_ref, out_ref, acc_ref):
     row_blocks = acc_ref.shape[0] - 1
     acc_ref[...] = jnp.zeros_like(acc_ref)
-    unroll = 36
+    unroll = tiles_ref.shape[0]
     columns = ext_ref.shape[1]
 
     @pl.loop(0, tiles_ref.shape[0] // unroll)

time: 35.1 us -> 35.2 us (level)
    pallas_call x1, Pallas kernels: 31.8 us -> 32.3 us  [local(): pl.pallas_call(functools.partial(exchange_kernel, n_dom, n_feat, cols, ch...]
where the time goes in v8:
time: 35.2 us; the launch traced here: 35.1 us
  Pallas kernels  34.4 us (98%)
  between operations  0.66 us (2%)
    pallas_call x1, Pallas kernels, local(): pl.pallas_call(functools.partial(exchange_kernel, n_dom, n_feat, cols, ch...  32.3 us
    pallas_call x1, Pallas kernels, local(): pl.pallas_call(tile_kernel, out_shape=shape((cols, rows), BF16), in_specs...  2.16 us

profile of v8, /device:TPU:1, one launch (start us, length us, event | category | flops | bytes accessed | tf_op | source)
XLA Modules:
  0.0 35.1 jit_solution(12206628205170064855)
XLA Ops:
  0.7 32.3 %exchange.1 = (bf16[88,32,128]{2,1,0:T(8,128)(2,1)S(1)}, bf16[108,128,128]{2,1,0:T(8,128)(2,1)S(1)}, s32[8,128]{1,0:T(8,128)S(4)}, f32[32,128]{1,0:T(8,128)S(1)}) custom-call(bf16[76,2048]{1,0:T(8,128)(2,1)} %bitcast.7, bf16[608,256]{1,0:T(8,128)(2,1)} %w_hbm.1, s32[8,1024]{1,0:T(8,128)} %bitcast.8, s32[8,128]{1,0:T(8,128)} %bitcast.9, ...), custom_call_target="tpu_custom_call" | custom-call | tf_op jit(solution)/shard_map/exchange/pallas_call | solution.py:424
  32.9 2.2 %tiles.1 = bf16[32,2048]{1,0:T(8,128)(2,1)} custom-call(s32[8,128]{1,0:T(8,128)S(4)} %get-tuple-element.9.meta_ref, bf16[108,128,128]{2,1,0:T(8,128)(2,1)S(1)} %get-tuple-element.10.tiles_ref, bf16[88,32,128]{2,1,0:T(8,128)(2,1)S(1)} %get-tuple-element.11.ext_ref, f32[32,128]{1,0:T(8,128)S(1)} %get-tuple-element.12.bias_ref), custom_call_target="tpu_custom_call" | custom-call | tf_op jit(solution)/shard_map/tiles/pallas_call | solution.py:479

commit v9 on v8

--- a/solution.py
+++ b/solution.py
@@ -253,17 +253,18 @@
 
     packed = Y_RING * HUB_MOST
 
-    def bulk(h):
+    def bulk(h, part=None):
         span = slice(h * chunk, (h + 1) * chunk)
-        arrived_in(rx.at[h], sxr.at[h])
+        if part != 1:
+            arrived_in(rx.at[h], sxr.at[h])
         total = sx[j, h].astype(F32)
         for d in range(1, n_feat):
             total = total + rx[h, d - 1].astype(F32)
         proj = total.astype(BF16)
-        for b in range(own_blocks):
+        for b in range(0 if part == 1 else own_blocks):
             ext_ref[b, span, :] = proj[:, b * BLK : (b + 1) * BLK]
         stacked = jnp.concatenate([proj[:, g * LO : (g + 1) * LO] for g in range(his)], 0)
-        for s in SEND_ORDER:
+        for s in SEND_ORDER if part is None else SEND_ORDER[4 * part : 4 * part + 4]:
             hi = lax.div(send_ref[s : s + 1, :], LO)
             rows_out = pick_groups(dot(stacked, hot_ref[s]), hi, his, chunk).astype(BF16)
             for b in range(slot_blocks):
@@ -291,7 +292,7 @@
             if other != ring_desk:
                 tell(ring_in, p, other)
 
-    bulk(1)
+    bulk(1, 0)
 
     arrived_in(hy.at[0 : Y_RING - 1], hyr)
     arrived = [hy[source].astype(F32) for source in range(Y_RING)]
@@ -325,6 +326,7 @@
         )
         copy.start()
 
+    bulk(1, 1)
     for h in range(2, n_chunk):
         bulk(h)
 

time: 35.2 us -> 33.6 us (0.955)
  Pallas kernels: 34.4 us -> 32.8 us
    pallas_call x1, Pallas kernels: 32.3 us -> 30.7 us  [local(): pl.pallas_call(functools.partial(exchange_kernel, n_dom, n_feat, cols, ch...]
where the time goes in v9:
time: 33.6 us; the launch traced here: 33.4 us
  Pallas kernels  32.8 us (98%)
  between operations  0.66 us (2%)
    pallas_call x1, Pallas kernels, local(): pl.pallas_call(functools.partial(exchange_kernel, n_dom, n_feat, cols, ch...  30.7 us
    pallas_call x1, Pallas kernels, local(): pl.pallas_call(tile_kernel, out_shape=shape((cols, rows), BF16), in_specs...  2.11 us

profile of v9, /device:TPU:1, one launch (start us, length us, event | category | flops | bytes accessed | tf_op | source)
XLA Modules:
  0.0 33.4 jit_solution(5395602532895779590)
XLA Ops:
  0.7 30.7 %exchange.1 = (bf16[88,32,128]{2,1,0:T(8,128)(2,1)S(1)}, bf16[108,128,128]{2,1,0:T(8,128)(2,1)S(1)}, s32[8,128]{1,0:T(8,128)S(4)}, f32[32,128]{1,0:T(8,128)S(1)}) custom-call(bf16[76,2048]{1,0:T(8,128)(2,1)} %bitcast.7, bf16[608,256]{1,0:T(8,128)(2,1)} %w_hbm.1, s32[8,1024]{1,0:T(8,128)} %bitcast.8, s32[8,128]{1,0:T(8,128)} %bitcast.9, ...), custom_call_target="tpu_custom_call" | custom-call | tf_op jit(solution)/shard_map/exchange/pallas_call | solution.py:426
  31.3 2.1 %tiles.1 = bf16[32,2048]{1,0:T(8,128)(2,1)} custom-call(s32[8,128]{1,0:T(8,128)S(4)} %get-tuple-element.9.meta_ref, bf16[108,128,128]{2,1,0:T(8,128)(2,1)S(1)} %get-tuple-element.10.tiles_ref, bf16[88,32,128]{2,1,0:T(8,128)(2,1)S(1)} %get-tuple-element.11.ext_ref, f32[32,128]{1,0:T(8,128)S(1)} %get-tuple-element.12.bias_ref), custom_call_target="tpu_custom_call" | custom-call | tf_op jit(solution)/shard_map/tiles/pallas_call | solution.py:481

commit v10 on v9

--- a/solution.py
+++ b/solution.py
@@ -315,12 +315,14 @@
     def _():
         pl.semaphore_wait(ring_in, 1)
 
+    near_z = [d for d in range(1, z_ring) if min(d, z_ring - d) <= z_ring // 4]
+    far_z = [d for d in range(1, z_ring) if d not in near_z]
     for d in far_first(z_ring):
         copy = pltpu.make_async_remote_copy(
             src_ref=hpack,
             dst_ref=hz.at[z],
             send_sem=hzs,
-            recv_sem=hzr,
+            recv_sem=hzr.at[0 if d in near_z else 1],
             device_id={"dom": z_at(d)},
             device_id_type=MESH,
         )
@@ -358,9 +360,14 @@
             first = own_blocks + s * slot_blocks
             ext_ref[first : first + slot_blocks] = jnp.zeros((slot_blocks, cols, BLK), BF16)
 
-    arrived_in(hz.at[0 : z_ring - 1], hzr)
-    everyone = jnp.concatenate([hz[source] for source in range(z_ring)], 0)
-    hub_block = pick_groups(dot(everyone, endhot_ref[...]), end_z, z_ring, cols).astype(BF16)
+    hub_block = jnp.zeros((cols, hubs), F32)
+    for group, steps in enumerate((near_z, far_z)):
+        arrived_in(hz.at[0 : len(steps)], hzr.at[group])
+        sources = [lax.rem(z + z_ring - d, z_ring) for d in ([0] if group == 0 else []) + steps]
+        found = dot(jnp.concatenate([hz[source] for source in sources], 0), endhot_ref[...])
+        for k, source in enumerate(sources):
+            hub_block = jnp.where(end_z == source, found[k * cols : (k + 1) * cols], hub_block)
+    hub_block = hub_block.astype(BF16)
     for b in range(hubs // BLK):
         ext_ref[hub_first + b] = hub_block[:, b * BLK : (b + 1) * BLK]
 
@@ -463,7 +470,7 @@
             dma,
             dma,
             dma,
-            dma,
+            dma((2,)),
             pltpu.SemaphoreType.REGULAR,
             pltpu.SemaphoreType.REGULAR,
             pltpu.SemaphoreType.REGULAR,

time: 33.6 us -> 33.8 us (level)
  no operation moved by 1% of the time
where the time goes in v10:
time: 33.8 us; the launch traced here: 33.6 us
  Pallas kernels  32.9 us (97%)
  between operations  0.66 us (2%)
    pallas_call x1, Pallas kernels, local(): pl.pallas_call(functools.partial(exchange_kernel, n_dom, n_feat, cols, ch...  30.9 us
    pallas_call x1, Pallas kernels, local(): pl.pallas_call(tile_kernel, out_shape=shape((cols, rows), BF16), in_specs...  2.06 us

profile of v10, /device:TPU:1, one launch (start us, length us, event | category | flops | bytes accessed | tf_op | source)
XLA Modules:
  0.0 33.6 jit_solution(12548286860255307087)
XLA Ops:
  0.7 30.9 %exchange.1 = (bf16[88,32,128]{2,1,0:T(8,128)(2,1)S(1)}, bf16[108,128,128]{2,1,0:T(8,128)(2,1)S(1)}, s32[8,128]{1,0:T(8,128)S(4)}, f32[32,128]{1,0:T(8,128)S(1)}) custom-call(bf16[76,2048]{1,0:T(8,128)(2,1)} %bitcast.7, bf16[608,256]{1,0:T(8,128)(2,1)} %w_hbm.1, s32[8,1024]{1,0:T(8,128)} %bitcast.8, s32[8,128]{1,0:T(8,128)} %bitcast.9, ...), custom_call_target="tpu_custom_call" | custom-call | tf_op jit(solution)/shard_map/exchange/pallas_call | solution.py:433
  31.5 2.1 %tiles.1 = bf16[32,2048]{1,0:T(8,128)(2,1)} custom-call(s32[8,128]{1,0:T(8,128)S(4)} %get-tuple-element.9.meta_ref, bf16[108,128,128]{2,1,0:T(8,128)(2,1)S(1)} %get-tuple-element.10.tiles_ref, bf16[88,32,128]{2,1,0:T(8,128)(2,1)S(1)} %get-tuple-element.11.ext_ref, f32[32,128]{1,0:T(8,128)S(1)} %get-tuple-element.12.bias_ref), custom_call_target="tpu_custom_call" | custom-call | tf_op jit(solution)/shard_map/tiles/pallas_call | solution.py:488
